TPU v7x, 128 devices: a whole 4x4x4 slice. The times are simulated.
128 devices in a mesh: rep: 2 (over y_lo), own: 64 (over x, z, y_hi, core).
Axes of the slice: x: 4, y: 4 (y_hi: 2, y_lo: 2; y = y_hi * 2 + y_lo), z: 4, core: 2. Of those that a mesh axis runs over, the one named last changes fastest.
Arguments:
- values: float32 [1048576, 128], P(('rep', 'own')), may hold values from -0.8 to 0.8
- key_ids: int32 [1048576], P(('rep', 'own')), may hold values from 0 to 262143, as said below
- heavy_ids: int32 [2048], replicated, may hold values from 0 to 262143, as said below
- block_offsets: int32 [128, 64], P(('rep', 'own')), may hold values from 0 to 8191, as said below
- block_counts: int32 [128, 64], P(('rep', 'own')), may hold values from 8 to 64, as said below
Outputs:
- light_sums: float32 [262144, 128], P('own')
- heavy_sums: float32 [2048, 128], P('own')
Inputs may be any that keep to these rules, and one draw needn't show every extreme that they name: `key_ids`: an event in block o of a device has a key in o * 4096 to (o + 1) * 4096 - 1 that is not a heavy key; every event outside all blocks has a heavy key. `heavy_ids`: distinct keys. `block_offsets`: on each device the blocks lie in the order of o, do not meet, and end by position 8192. `block_counts`: at most 64; one owner gets exactly 64 from every device.
All inputs are finite; a program needn't handle non-finite values.
Results may differ from a plain program's by a relative error of at most 0.000075.
Values sent between devices are 32-bit elements; how exact they have to be, the bound alone decides.
No kernel may reach another device: no remote copies, remote signals or barrier semaphores. Data moves between devices by JAX's collectives and lax.ppermute only.
A program may use at most 64 MiB of HBM per device.

v0:
```python
import math

import jax
import jax.numpy as jnp
from jax import lax
from jax.sharding import PartitionSpec as P

KEYS_DEV = 4096
CAP = 64


def over_pieces(x, axis):
    blocks = lax.all_gather(x, axis)
    return blocks.sum(axis=0)


def in_blocks(x, dim, size):
    lengths = x.shape
    blocks = x.reshape(*lengths[:dim], size, lengths[dim] // size, *lengths[dim + 1 :])
    return jnp.moveaxis(blocks, dim, 0)


def sum_at_owner(x, axis, dim):
    size = lax.axis_size(axis)
    blocks = lax.all_to_all(in_blocks(x, dim, size), axis, 0, 0, tiled=True)
    return jnp.sum(blocks, axis=0)


def key_sums(rows_in, row_keys, targets):
    slots = row_keys.shape[0]
    block_len = math.gcd(slots, 2048)
    count_blocks = slots // block_len
    rows_blocks = rows_in.reshape(count_blocks, block_len, rows_in.shape[1])
    keys_blocks = row_keys.reshape(count_blocks, block_len)

    def accumulate(running, pieces):
        rows_piece, keys_piece = pieces
        onehot = (targets[:, None] == keys_piece[None, :]).astype(jnp.float32)
        added = jnp.dot(
            onehot, rows_piece, precision=lax.Precision.HIGHEST, preferred_element_type=jnp.float32
        )
        return (running + added, None)

    start_sums = jnp.zeros((targets.shape[0], rows_in.shape[1]), jnp.float32)
    running, unused = lax.scan(accumulate, start_sums, (rows_blocks, keys_blocks))
    return running


def per_device(values, key_ids, heavy_ids, block_offsets, block_counts):
    owners = lax.axis_size("own")
    pairs = lax.axis_size("rep")
    own_index = lax.axis_index("own")
    rep_index = lax.axis_index("rep")
    width = values.shape[1]
    slot_cap = CAP
    padded_values = jnp.concatenate([values, jnp.zeros((slot_cap, width), jnp.float32)], axis=0)
    padded_keys = jnp.concatenate([key_ids, jnp.full((slot_cap,), -1, jnp.int32)], axis=0)
    slot_iota = jnp.arange(slot_cap, dtype=jnp.int32)
    positions = block_offsets[0][:, None] + slot_iota[None, :]
    valid = slot_iota[None, :] < block_counts[0][:, None]
    block_rows = jnp.where(valid[:, :, None], jnp.take(padded_values, positions, axis=0), 0.0)
    block_keys = jnp.where(valid, jnp.take(padded_keys, positions, axis=0), -1)
    half_keys = KEYS_DEV // 2
    owner_base = (jnp.arange(owners, dtype=jnp.int32) * KEYS_DEV)[:, None]
    which_half = jnp.where(block_keys >= 0, (block_keys - owner_base) // half_keys, -1)
    split_rows = jnp.stack(
        [jnp.where((which_half == side)[:, :, None], block_rows, 0.0) for side in range(pairs)],
        axis=0,
    )
    split_keys = jnp.stack(
        [jnp.where(which_half == side, block_keys, -1) for side in range(pairs)], axis=0
    )
    split_rows = split_rows.reshape(pairs * owners, slot_cap, width)
    split_keys = split_keys.reshape(pairs * owners, slot_cap)
    got_rows, got_keys = (
        lax.all_to_all(split_rows, ("rep", "own"), split_axis=0, concat_axis=0, tiled=True),
        lax.all_to_all(split_keys, ("rep", "own"), split_axis=0, concat_axis=0, tiled=True),
    )
    local_keys = jnp.where(
        got_keys >= 0, got_keys - own_index * KEYS_DEV - rep_index * half_keys, -1
    ).reshape(-1)
    owned_half = key_sums(
        got_rows.reshape(-1, width), local_keys, jnp.arange(half_keys, dtype=jnp.int32)
    )
    light_sums = lax.all_gather(owned_half, "rep", axis=0, tiled=True)
    partial_sums = key_sums(values, key_ids, heavy_ids)
    summed_pair = over_pieces(partial_sums, "rep")
    heavy_sums = sum_at_owner(summed_pair, "own", 0)
    return (light_sums, heavy_sums)


def solution(mesh):
    placed = (
        P(("rep", "own"), None),
        P(("rep", "own")),
        P(),
        P(("rep", "own"), None),
        P(("rep", "own"), None),
    )
    return jax.shard_map(
        per_device,
        mesh=mesh,
        in_specs=placed,
        out_specs=(P("own", None), P("own", None)),
        check_vma=False,
    )
```

profile of v0, /device:TPU:1, one launch (start us, length us, event | category | flops | bytes accessed | tf_op | source)
XLA Modules:
  0.0 223.6 jit_solution(12802448935710163705)
XLA Ops:
  7.2 0.7 compare_select_fusion.2
  7.9 0.1 reshape.542
  8.0 0.8 concatenate.6
  8.8 0.0 copy-start.3
  8.8 23.0 %gather_fusion = s32[4096]{0:T(1024)S(1)} fusion(s32[8256]{0:T(1024)S(1)} %concatenate.6, s32[4096]{0:T(1024)S(1)} %broadcast_clamp_fusion), kind=kCustom, calls=%fused_computation | custom fusion | bytes 49152 | tf_op jit(solution)/shard_map/jit(_take)/gather | solution.py:62
  31.8 0.1 gather.13
  31.9 0.0 copy-done.3
  31.9 0.0 copy-done.4
  31.9 0.1 compare_select_fusion.5
  32.0 0.6 pad_add_fusion
  32.6 11.5 %all-to-all-start = ((s32[128,1,64]{2,1,0:T(1,128)}), s32[128,1,64]{2,1,0:T(1,128)S(1)}, u32[]{:S(2)}, u32[]{:S(2)}) async-start(s32[128,1,64]{2,1,0:T(1,128)} %bitcast.2), calls=%async_computation | async-start | bytes 131072 | tf_op jit(solution)/shard_map/all_to_all | solution.py:77
  44.1 0.1 reshape.541
  44.2 0.1 broadcast_compare_fusion.1
  44.3 3.7 %concatenate.7 = f32[8256,128]{1,0:T(8,128)} pad(f32[8192,128]{1,0:T(8,128)} %param.9, f32[]{:T(128)} %constant.53.clone.1), padding=0_64x0_0 | pad | bytes 8421380 | tf_op jit(solution)/shard_map/concatenate | solution.py:56
  48.0 13.0 %gather_fusion.1 = f32[4096,128]{1,0:T(8,128)S(1)} fusion(f32[8256,128]{1,0:T(8,128)} %concatenate.7, s32[4096]{0:T(1024)S(1)} %broadcast_clamp_fusion), kind=kCustom, calls=%fused_computation.1 | custom fusion | bytes 4210688 | tf_op jit(solution)/shard_map/jit(_take)/gather | solution.py:61
  61.0 2.5 %fusion.19 = (f32[1,64,64,128]{3,2,1,0:T(8,128)S(1)}, f32[1,64,64,128]{3,2,1,0:T(8,128)S(1)}) fusion(f32[1,64,64,128]{3,2,1,0:T(8,128)S(1)} %bitcast.28, pred[64,64]{1,0:T(8,128)(4,1)S(1)} %get-tuple-element.118, pred[64,64]{1,0:T(8,128)(4,1)S(1)} %get-tuple-element.117, pred[64,64]{1,0:T(8,128)(4,1)S(1)} %get-tuple-element.111, ...), kind=kLoop, calls=%fused_computation.23 | loop fusion | flops 2097152 | bytes 6307840 | tf_op jit(solution)/shard_map/jit(_where)/select_n | solution.py:67
  63.5 2.3 %pad_maximum_fusion = f32[2,64,64,128]{3,2,1,0:T(8,128)} fusion(f32[1,64,64,128]{3,2,1,0:T(8,128)S(1)} %get-tuple-element.114, f32[1,64,64,128]{3,2,1,0:T(8,128)S(1)} %get-tuple-element.113), kind=kLoop, calls=%fused_computation.20 | loop fusion | flops 1048576 | bytes 8388608 | tf_op jit(solution)/shard_map/stack | solution.py:66
  65.8 0.0 all-to-all-done
  65.8 10.2 %all-to-all-start.1 = ((f32[128,64,128]{2,1,0:T(8,128)}), f32[128,64,128]{2,1,0:T(8,128)}, u32[]{:S(2)}, u32[]{:S(2)}) async-start(f32[128,64,128]{2,1,0:T(8,128)} %bitcast.27), calls=%async_computation.1 | async-start | bytes 8388608 | tf_op jit(solution)/shard_map/all_to_all | solution.py:76
  76.0 0.0 all-gather.6.cloned.1.call-start
  76.0 0.0 copy-done.2
  76.1 0.0 copy-done.5
  76.1 34.5 %while.23 = (s32[]{:T(128)}, f32[2048,128]{1,0:T(8,128)S(1)}, s32[2048]{0:T(1024)S(1)}, s32[4,2048]{1,0:T(4,128)S(1)}, f32[4,2048,128]{2,1,0:T(8,128)}, /*index=5*/s32[]{:T(128)}, s32[]{:T(128)}) while((s32[]{:T(128)}, f32[2048,128]{1,0:T(8,128)S(1)}, s32[2048]{0:T(1024)S(1)}, s32[4,2048]{1,0:T(4,128)S(1)}, ...), condition=%wide.region_3.4_spmd.clone, body=%wide.region_2.3_spmd.clone.sunk | while | flops 6447169536 | bytes 3179099 | solution.py:45
  76.1 8.6 %fusion.43 = f32[2048,128]{1,0:T(8,128)S(1)} fusion(s32[2048]{0:T(1024)S(1)} %bitcast.32, s32[2048]{0:T(1024)S(1)} %get-tuple-element.209, f32[2048,128]{1,0:T(8,128)S(1)} %get-tuple-element.201, f32[4,2048,128]{2,1,0:T(8,128)} %get-tuple-element.211, s32[]{:T(128)} %get-tuple-element.200, pred[]{:T(512)S(6)} %compare.33), kind=kOutput, calls=%fused_computation.15.clone.1 | convolution fusion | flops 6447169536 | bytes 3162625 | tf_op jit(solution)/shard_map/while/body/eval_jaxpr/dot_general | solution.py:39
  84.7 8.6 %fusion.43 = f32[2048,128]{1,0:T(8,128)S(1)} fusion(s32[2048]{0:T(1024)S(1)} %bitcast.32, s32[2048]{0:T(1024)S(1)} %get-tuple-element.209, f32[2048,128]{1,0:T(8,128)S(1)} %get-tuple-element.201, f32[4,2048,128]{2,1,0:T(8,128)} %get-tuple-element.211, s32[]{:T(128)} %get-tuple-element.200, pred[]{:T(512)S(6)} %compare.33), kind=kOutput, calls=%fused_computation.15.clone.1 | convolution fusion | flops 6447169536 | bytes 3162625 | tf_op jit(solution)/shard_map/while/body/eval_jaxpr/dot_general | solution.py:39
  93.4 8.6 %fusion.43 = f32[2048,128]{1,0:T(8,128)S(1)} fusion(s32[2048]{0:T(1024)S(1)} %bitcast.32, s32[2048]{0:T(1024)S(1)} %get-tuple-element.209, f32[2048,128]{1,0:T(8,128)S(1)} %get-tuple-element.201, f32[4,2048,128]{2,1,0:T(8,128)} %get-tuple-element.211, s32[]{:T(128)} %get-tuple-element.200, pred[]{:T(512)S(6)} %compare.33), kind=kOutput, calls=%fused_computation.15.clone.1 | convolution fusion | flops 6447169536 | bytes 3162625 | tf_op jit(solution)/shard_map/while/body/eval_jaxpr/dot_general | solution.py:39
  102.0 8.6 %fusion.43 = f32[2048,128]{1,0:T(8,128)S(1)} fusion(s32[2048]{0:T(1024)S(1)} %bitcast.32, s32[2048]{0:T(1024)S(1)} %get-tuple-element.209, f32[2048,128]{1,0:T(8,128)S(1)} %get-tuple-element.201, f32[4,2048,128]{2,1,0:T(8,128)} %get-tuple-element.211, s32[]{:T(128)} %get-tuple-element.200, pred[]{:T(512)S(6)} %compare.33), kind=kOutput, calls=%fused_computation.15.clone.1 | convolution fusion | flops 6447169536 | bytes 3162625 | tf_op jit(solution)/shard_map/while/body/eval_jaxpr/dot_general | solution.py:39
  110.6 0.0 copy-start.1
  110.6 1.0 copy-done.1
  111.6 0.0 all-gather.6.cloned.1.call-update
  111.6 0.2 all-gather.4.cloned.1.call-start
  111.8 0.2 fusion.20
  112.1 0.1 select_n.219
  112.2 17.3 %all-to-all-done.1 = f32[128,64,128]{2,1,0:T(8,128)} async-done(((f32[128,64,128]{2,1,0:T(8,128)}), f32[128,64,128]{2,1,0:T(8,128)}, u32[]{:S(2)}, u32[]{:S(2)}) %all-to-all-start.1) | async-done | bytes 4194336 | tf_op jit(solution)/shard_map/all_to_all | solution.py:76
  129.4 36.5 %while.22 = (s32[]{:T(128)}, f32[2048,128]{1,0:T(8,128)S(1)}, s32[4,2048]{1,0:T(4,128)S(1)}, f32[4,2048,128]{2,1,0:T(8,128)}, s32[]{:T(128)}, /*index=5*/s32[]{:T(128)}) while((s32[]{:T(128)}, f32[2048,128]{1,0:T(8,128)S(1)}, s32[4,2048]{1,0:T(4,128)S(1)}, f32[4,2048,128]{2,1,0:T(8,128)}, s32[]{:T(128)}, /*index=5*/s32[]{:T(128)}) %tuple.48), condition=%wide.region_1.2_spmd.clone, body=%wide.region_0.1_spmd.clone.sunk | while | flops 6447169536 | bytes 3170899 | solution.py:45
  129.5 9.1 %fusion.40 = f32[2048,128]{1,0:T(8,128)S(1)} fusion(s32[2048]{0:T(1024)S(1)} %bitcast.33, f32[2048,128]{1,0:T(8,128)S(1)} %get-tuple-element.182, f32[4,2048,128]{2,1,0:T(8,128)} %get-tuple-element.190, s32[]{:T(128)} %get-tuple-element.181, pred[]{:T(512)S(6)} %compare.32), kind=kOutput, calls=%fused_computation.6.clone.1 | convolution fusion | flops 6447169536 | bytes 3154433 | tf_op jit(solution)/shard_map/while/body/eval_jaxpr/dot_general | solution.py:39
  138.6 9.1 %fusion.40 = f32[2048,128]{1,0:T(8,128)S(1)} fusion(s32[2048]{0:T(1024)S(1)} %bitcast.33, f32[2048,128]{1,0:T(8,128)S(1)} %get-tuple-element.182, f32[4,2048,128]{2,1,0:T(8,128)} %get-tuple-element.190, s32[]{:T(128)} %get-tuple-element.181, pred[]{:T(512)S(6)} %compare.32), kind=kOutput, calls=%fused_computation.6.clone.1 | convolution fusion | flops 6447169536 | bytes 3154433 | tf_op jit(solution)/shard_map/while/body/eval_jaxpr/dot_general | solution.py:39
  147.7 9.1 %fusion.40 = f32[2048,128]{1,0:T(8,128)S(1)} fusion(s32[2048]{0:T(1024)S(1)} %bitcast.33, f32[2048,128]{1,0:T(8,128)S(1)} %get-tuple-element.182, f32[4,2048,128]{2,1,0:T(8,128)} %get-tuple-element.190, s32[]{:T(128)} %get-tuple-element.181, pred[]{:T(512)S(6)} %compare.32), kind=kOutput, calls=%fused_computation.6.clone.1 | convolution fusion | flops 6447169536 | bytes 3154433 | tf_op jit(solution)/shard_map/while/body/eval_jaxpr/dot_general | solution.py:39
  156.9 9.1 %fusion.40 = f32[2048,128]{1,0:T(8,128)S(1)} fusion(s32[2048]{0:T(1024)S(1)} %bitcast.33, f32[2048,128]{1,0:T(8,128)S(1)} %get-tuple-element.182, f32[4,2048,128]{2,1,0:T(8,128)} %get-tuple-element.190, s32[]{:T(128)} %get-tuple-element.181, pred[]{:T(512)S(6)} %compare.32), kind=kOutput, calls=%fused_computation.6.clone.1 | convolution fusion | flops 6447169536 | bytes 3154433 | tf_op jit(solution)/shard_map/while/body/eval_jaxpr/dot_general | solution.py:39
  166.0 0.0 copy-start
  166.0 1.0 copy-done
  167.0 0.0 all-gather.4.cloned.1.call-update
  167.0 0.0 all-gather.6.cloned.1.call-done
  167.0 1.8 reduce_sum.18
  168.9 30.6 %all_to_all.19 = f32[64,32,128]{2,1,0:T(8,128)S(1)} all-to-all(f32[64,32,128]{2,1,0:T(8,128)S(1)} %bitcast.30), channel_id=1, replica_groups=mesh['rep'=2,'own'=64] {'own'}, dimensions={0} | all-to-all | bytes 2097152 | tf_op jit(solution)/shard_map/all_to_all | solution.py:25
  199.4 0.7 reduce_sum.19
  200.1 13.6 %all-gather.4.cloned.1.call-done = f32[4096,128]{1,0:T(8,128)} async-done(((f32[2048,128]{1,0:T(8,128)}), f32[4096,128]{1,0:T(8,128)}) %all-gather.4.cloned.1.call-update) | async-done | bytes 2097168 | tf_op jit(solution)/shard_map/all_gather | solution.py:85
  213.7 3.0 %copy.20 = f32[4096,128]{1,0:T(8,128)} copy(f32[4096,128]{1,0:T(8,128)} %all-gather.4.cloned.1.call-done) | data formatting | bytes 4194304
  (17 shorter events, 0.1 us)
Async XLA Ops:
  8.8 23.1 %copy-start.3 = (s32[1,64]{1,0:T(1,128)S(1)}, s32[1,64]{1,0:T(1,128)}, u32[]{:S(2)}) copy-start(s32[1,64]{1,0:T(1,128)} %param.12) | copy-start | bytes 772
  8.8 23.1 %copy-start.4 = (s32[1,64]{1,0:T(1,128)S(1)}, s32[1,64]{1,0:T(1,128)}, u32[]{:S(2)}) copy-start(s32[1,64]{1,0:T(1,128)} %param.13) | copy-start | bytes 772
  32.6 33.1 %all-to-all-start = ((s32[128,1,64]{2,1,0:T(1,128)}), s32[128,1,64]{2,1,0:T(1,128)S(1)}, u32[]{:S(2)}, u32[]{:S(2)}) async-start(s32[128,1,64]{2,1,0:T(1,128)} %bitcast.2), calls=%async_computation | async-start | bytes 131072 | tf_op jit(solution)/shard_map/all_to_all | solution.py:77
  65.8 10.3 %copy-start.2 = (s32[8192]{0:T(1024)S(1)}, s32[8192]{0:T(1024)}, u32[]{:S(2)}) copy-start(s32[8192]{0:T(1024)} %param.10) | copy-start | bytes 98308
  65.8 10.3 %copy-start.5 = (s32[2048]{0:T(1024)S(1)}, s32[2048]{0:T(1024)}, u32[]{:S(2)}) copy-start(s32[2048]{0:T(1024)} %param.11) | copy-start | bytes 24580
  65.8 63.7 %all-to-all-start.1 = ((f32[128,64,128]{2,1,0:T(8,128)}), f32[128,64,128]{2,1,0:T(8,128)}, u32[]{:S(2)}, u32[]{:S(2)}) async-start(f32[128,64,128]{2,1,0:T(8,128)} %bitcast.27), calls=%async_computation.1 | async-start | bytes 8388608 | tf_op jit(solution)/shard_map/all_to_all | solution.py:76
  76.0 91.0 %all-gather.6.cloned.1.call-start = ((), (), s32[]{:S(2)}) async-start(), calls=%async_computation.4 | async-start | bytes 3145728 | tf_op jit(solution)/shard_map/all_gather | solution.py:13
  110.6 1.0 copy-start.1
  111.6 102.1 %all-gather.4.cloned.1.call-start = ((), (), s32[]{:S(2)}) async-start(), calls=%async_computation.3 | async-start | bytes 3145728 | tf_op jit(solution)/shard_map/all_gather | solution.py:85
  166.0 1.0 copy-start
Sparse Core Ops, SparseCore 0:
  111.7 36.9 all-gather.5
  167.1 46.5 all-gather.3
where the time goes:
time: 224 us
  matrix products  70.7 us (32%)
  local copies, waits for them, and re-layouts  45.9 us (20%)
  waiting for transfers between devices  31 us (14%)
  blocking collectives  30.6 us (14%)
  starting transfers between devices  22 us (10%)
  between operations  14.2 us (6%)
  other arithmetic  9.15 us (4%)
    dot_general x8, matrix products, accumulate(): jnp.dot(onehot, rows_piece, precision=lax.Precision.HIGHEST, preferred_el...  70.7 us
    all_to_all x1, blocking collectives, sum_at_owner(): blocks = lax.all_to_all(in_blocks(x, dim, size), axis, 0, 0, tiled=True)  30.6 us
    gather x3, local copies, waits for them, and re-layouts, per_device(): block_keys = jnp.where(valid, jnp.take(padded_keys, positions, axis=0), -1)  23.2 us
    all_to_all x1, waiting for transfers between devices, per_device(): lax.all_to_all(split_rows, ('rep', 'own'), split_axis=0, concat_axis=0, t...  17.3 us
    all_gather x1, waiting for transfers between devices, per_device(): light_sums = lax.all_gather(owned_half, 'rep', axis=0, tiled=True)  13.6 us
    gather x1, local copies, waits for them, and re-layouts, per_device(): jnp.take(padded_values, positions, axis=0)  13 us
    all_to_all x1, starting transfers between devices, per_device(): lax.all_to_all(split_keys, ('rep', 'own'), split_axis=0, concat_axis=0, t...  11.5 us
    all_to_all x1, starting transfers between devices, per_device(): lax.all_to_all(split_rows, ('rep', 'own'), split_axis=0, concat_axis=0, t...  10.2 us
  transfers between devices with their start and end apart: 4, of which 2 were waited for; matrix products, arithmetic and copies ran while one was open for 43% of the time, Pallas kernels for 0%

commit v1 on v0

v1 whole, which is shorter than its diff:
```python
import jax
import jax.numpy as jnp
from jax import lax
from jax.experimental import pallas as pl
from jax.experimental.pallas import tpu as pltpu
from jax.sharding import PartitionSpec as P

KEYS_DEV = 4096
CAP = 64
LANES = 128
BANKS = 8
CHUNK = 32


def pack_blocks(offs, cnts, keys, values, owners, reps):
    events, width = values.shape
    key_rows = events // LANES
    block = CAP + 1

    def body(off_ref, cnt_ref, keys_ref, val_ref, out_ref, buf, krow, arow, sem):
        lane = lax.broadcasted_iota(jnp.int32, (1, LANES), 1)

        def step(o, carry):
            off = off_ref[0, o]
            cnt = cnt_ref[0, o]
            start = jnp.minimum(off, events - CAP)
            row = start // LANES
            shift = start - row * LANES
            row_next = jnp.minimum(row + 1, key_rows - 1)
            first = lane >= shift
            pos = jnp.where(first, row * LANES + lane, (row + 1) * LANES + lane)
            key = jnp.where(first, keys_ref[pl.ds(row, 1), :], keys_ref[pl.ds(row_next, 1), :])
            inside = (pos >= off) & (pos < off + cnt)
            krow[pl.ds(o, 1), :] = jnp.where(inside, key - o * KEYS_DEV, KEYS_DEV)
            arow[pl.ds(o, 1), :] = jnp.full((1, LANES), shift, jnp.int32)
            buf[pl.ds(o * block, CAP), :] = val_ref[pl.ds(start, CAP), :]
            return carry

        lax.fori_loop(0, owners, step, 0, unroll=8)
        rolled = krow[...]
        shifts = arow[...]
        for bit in range(7):
            moved = pltpu.roll(rolled, LANES - (1 << bit), 1)
            rolled = jnp.where((shifts >> bit) & 1 == 1, moved, rolled)
        krow[...] = rolled
        for o in range(owners):
            buf[pl.ds(o * block + CAP, 1), :] = krow[pl.ds(o, 1), :].astype(jnp.float32)
        copies = [pltpu.make_async_copy(buf, out_ref.at[r], sem.at[r]) for r in range(reps)]
        for copy in copies:
            copy.start()
        for copy in copies:
            copy.wait()

    smem = pl.BlockSpec(memory_space=pltpu.SMEM)
    vmem = pl.BlockSpec(memory_space=pltpu.VMEM)
    packed = pl.pallas_call(
        body,
        out_shape=jax.ShapeDtypeStruct((reps, owners * block, width), jnp.float32),
        in_specs=[smem, smem, vmem, vmem],
        out_specs=pl.BlockSpec(memory_space=pl.ANY),
        scratch_shapes=[
            pltpu.VMEM((owners * block, width), jnp.float32),
            pltpu.VMEM((owners, LANES), jnp.int32),
            pltpu.VMEM((owners, LANES), jnp.int32),
            pltpu.SemaphoreType.DMA((reps,)),
        ],
        name="pack_blocks",
    )(offs, cnts, keys.reshape(key_rows, LANES), values)
    return packed.reshape(reps * owners, block, 1, width)


def light_kernel(recv):
    senders, block, _, width = recv.shape
    chunks = senders // CHUNK

    def body(recv_ref, out_ref, rows, kint, ksm, *rest):
        acc = rest[:BANKS]
        key_sem, smem_sem, row_sems = rest[BANKS:]
        key_copy = pltpu.make_async_copy(recv_ref.at[:, CAP], rows.at[:, CAP], key_sem)
        key_copy.start()
        copies = []
        for c in range(chunks):
            part = (pl.ds(c * CHUNK, CHUNK), pl.ds(0, CAP))
            copies.append(
                pltpu.make_async_copy(recv_ref.at[part], rows.at[part], row_sems.at[c])
            )
            copies[c].start()
        key_copy.wait()

        def convert(i, carry):
            kint[i] = rows[i, CAP].astype(jnp.int32)
            return carry

        lax.fori_loop(0, senders, convert, 0, unroll=8)
        smem_copy = pltpu.make_async_copy(kint, ksm, smem_sem)
        smem_copy.start()
        zeros = jnp.zeros((64, width), jnp.float32)

        def clear(i, carry):
            for bank in acc:
                bank[pl.ds(i * 64, 64), :] = zeros
            return carry

        lax.fori_loop(0, KEYS_DEV // 64, clear, 0)
        smem_copy.wait()

        def sender(i, carry):
            for s in range(CAP):
                bank = acc[s % BANKS]
                key = ksm[i, 0, s]
                bank[pl.ds(key, 1), :] = bank[pl.ds(key, 1), :] + rows[i, s]
            return carry

        for c in range(chunks):
            copies[c].wait()
            lax.fori_loop(c * CHUNK, (c + 1) * CHUNK, sender, 0)

        def finish(i, carry):
            span = pl.ds(i * 64, 64)
            total = acc[0][span, :]
            for bank in acc[1:]:
                total = total + bank[span, :]
            out_ref[span, :] = total
            return carry

        lax.fori_loop(0, KEYS_DEV // 64, finish, 0)

    return pl.pallas_call(
        body,
        out_shape=jax.ShapeDtypeStruct((KEYS_DEV, width), jnp.float32),
        in_specs=[pl.BlockSpec(memory_space=pl.ANY)],
        out_specs=pl.BlockSpec(memory_space=pltpu.VMEM),
        scratch_shapes=[
            pltpu.VMEM((senders, block, 1, width), jnp.float32),
            pltpu.VMEM((senders, 1, width), jnp.int32),
            pltpu.SMEM((senders, 1, width), jnp.int32),
        ]
        + [pltpu.VMEM((KEYS_DEV + 8, width), jnp.float32) for _ in range(BANKS)]
        + [
            pltpu.SemaphoreType.DMA,
            pltpu.SemaphoreType.DMA,
            pltpu.SemaphoreType.DMA((chunks,)),
        ],
        name="light_sums",
    )(recv)


def heavy_kernel(values, keys, heavy_ids):
    events, width = values.shape
    heavy = heavy_ids.shape[0]
    step_events = 2048
    tile = 512
    rows = step_events // LANES
    steps = events // step_events

    def body(h_ref, k_ref, v_ref, out_ref, ids, acc):
        c = pl.program_id(0)

        @pl.when(c == 0)
        def _():
            ids[...] = jnp.broadcast_to(h_ref[...], ids.shape)

        v = v_ref[...]
        high = v.astype(jnp.bfloat16)
        low = (v - high.astype(jnp.float32)).astype(jnp.bfloat16)
        rhs = jnp.concatenate([high, low], axis=1)
        key_rows = [k_ref[pl.ds(c * rows + j, 1), :] for j in range(rows)]
        for t in range(heavy // tile):
            span = pl.ds(t * tile, tile)
            h = ids[span, :]
            onehot = jnp.concatenate(
                [jnp.where(h == row, 1.0, 0.0).astype(jnp.bfloat16) for row in key_rows], axis=1
            )
            added = jnp.dot(onehot, rhs, preferred_element_type=jnp.float32)

            @pl.when(c == 0)
            def _():
                acc[span, :] = added

            @pl.when(c != 0)
            def _():
                acc[span, :] += added

        @pl.when(c == steps - 1)
        def _():
            out_ref[...] = acc[:, :width] + acc[:, width:]

    return pl.pallas_call(
        body,
        grid=(steps,),
        out_shape=jax.ShapeDtypeStruct((heavy, width), jnp.float32),
        in_specs=[
            pl.BlockSpec((heavy, 1), lambda c: (0, 0)),
            pl.BlockSpec((events // LANES, LANES), lambda c: (0, 0)),
            pl.BlockSpec((step_events, width), lambda c: (c, 0)),
        ],
        out_specs=pl.BlockSpec((heavy, width), lambda c: (0, 0)),
        scratch_shapes=[
            pltpu.VMEM((heavy, LANES), jnp.int32),
            pltpu.VMEM((heavy, 2 * width), jnp.float32),
        ],
        cost_estimate=pl.CostEstimate(
            flops=4 * events * heavy * width, bytes_accessed=4 * events * width, transcendentals=0
        ),
        name="heavy_sums",
    )(heavy_ids.reshape(heavy, 1), keys.reshape(events // LANES, LANES), values)


def per_device(values, key_ids, heavy_ids, block_offsets, block_counts):
    owners = lax.axis_size("own")
    pairs = lax.axis_size("rep")
    packed = pack_blocks(block_offsets, block_counts, key_ids, values, owners, pairs)
    recv = lax.all_to_all(packed, ("rep", "own"), split_axis=0, concat_axis=0, tiled=True)
    partial = heavy_kernel(values, key_ids, heavy_ids)
    heavy, width = partial.shape
    pieces = lax.all_to_all(
        partial.reshape(owners, heavy // owners, width), "own", 0, 0, tiled=True
    )
    mine = jnp.sum(pieces, axis=0)
    heavy_sums = mine + lax.ppermute(mine, "rep", [(0, 1), (1, 0)])
    light_sums = light_kernel(recv)
    return (light_sums, heavy_sums)


def solution(mesh):
    placed = (
        P(("rep", "own"), None),
        P(("rep", "own")),
        P(),
        P(("rep", "own"), None),
        P(("rep", "own"), None),
    )
    return jax.shard_map(
        per_device,
        mesh=mesh,
        in_specs=placed,
        out_specs=(P("own", None), P("own", None)),
        check_vma=False,
    )
```

time: 224 us -> 131 us (0.58)
  matrix products: 70.7 us -> 0 us
  local copies, waits for them, and re-layouts: 45.9 us -> 2.04 us
  Pallas kernels: 0 us -> 41 us
  waiting for transfers between devices: 31 us -> 66.6 us
  blocking collectives: 30.6 us -> 0 us
  between operations: 14.2 us -> 0.66 us
  other arithmetic: 9.15 us -> 0.71 us
  starting transfers between devices: 22 us -> 18.7 us
    dot_general x8 -> x0, matrix products: 70.7 us -> none  [accumulate(): jnp.dot(onehot, rows_piece, precision=lax.Precision.HIGHEST, preferred_el...]
    ppermute x0 -> x1, waiting for transfers between devices: none -> 47.9 us  [per_device(): heavy_sums = mine + lax.ppermute(mine, 'rep', [(0, 1), (1, 0)])]
    pallas_call x0 -> x3, Pallas kernels: none -> 41 us  [the longest x1 23.3 us: heavy_kernel(): pl.pallas_call(body, grid=(steps,), out_shape=jax.ShapeDtypeStruct((heavy...]
    gather x4 -> x0, local copies, waits for them, and re-layouts: 36.1 us -> none  [the longest x3 23.2 us: per_device(): block_keys = jnp.where(valid, jnp.take(padded_keys, positions, axis=0), -1)]
    all_to_all x1 -> x0, blocking collectives: 30.6 us -> none  [sum_at_owner(): blocks = lax.all_to_all(in_blocks(x, dim, size), axis, 0, 0, tiled=True)]
    all_gather x2 -> x0, waiting for transfers between devices: 13.6 us -> none  [the longest x1 13.6 us: per_device(): light_sums = lax.all_gather(owned_half, 'rep', axis=0, tiled=True)]
    unnamed x13 -> x0, local copies, waits for them, and re-layouts: 5.01 us -> none
    all_to_all x2, starting transfers between devices: 21.7 us -> 17.2 us  [the longest x1 12.5 us: per_device(): lax.all_to_all(partial.reshape(owners, heavy // owners, width), 'own', 0,...]
  transfers between devices with their start and end apart: 4 -> 3, of which waited for: 2 -> 3; matrix products, arithmetic and copies ran while one was open for 43% -> 1% of each run, Pallas kernels for 0% -> 4%
where the time goes in v1:
time: 131 us; the launch traced here: 130 us
  waiting for transfers between devices  66.6 us (51%)
  Pallas kernels  41 us (31%)
  starting transfers between devices  18.7 us (14%)
  local copies, waits for them, and re-layouts  2.04 us (2%)
    ppermute x1, waiting for transfers between devices, per_device(): heavy_sums = mine + lax.ppermute(mine, 'rep', [(0, 1), (1, 0)])  47.9 us
    pallas_call x1, Pallas kernels, heavy_kernel(): pl.pallas_call(body, grid=(steps,), out_shape=jax.ShapeDtypeStruct((heavy...  23.3 us
    all_to_all x1, waiting for transfers between devices, per_device(): lax.all_to_all(partial.reshape(owners, heavy // owners, width), 'own', 0,...  14.1 us
    all_to_all x1, starting transfers between devices, per_device(): lax.all_to_all(partial.reshape(owners, heavy // owners, width), 'own', 0,...  12.5 us
    pallas_call x1, Pallas kernels, light_kernel(): pl.pallas_call(body, out_shape=jax.ShapeDtypeStruct((KEYS_DEV, width), jn...  12.3 us
    pallas_call x1, Pallas kernels, pack_blocks(): pl.pallas_call(body, out_shape=jax.ShapeDtypeStruct((reps, owners * block...  5.33 us
    all_to_all x1, starting transfers between devices, per_device(): lax.all_to_all(packed, ('rep', 'own'), split_axis=0, concat_axis=0, tiled...  4.77 us
    all_to_all x1, waiting for transfers between devices, per_device(): lax.all_to_all(packed, ('rep', 'own'), split_axis=0, concat_axis=0, tiled...  4.56 us
  transfers between devices with their start and end apart: 3, of which 3 were waited for; matrix products, arithmetic and copies ran while one was open for 1% of the time, Pallas kernels for 4%

profile of v1, /device:TPU:1, one launch (start us, length us, event | category | flops | bytes accessed | tf_op | source)
XLA Modules:
  0.0 129.7 jit_solution(17073442961716742230)
XLA Ops:
  0.6 2.0 %copy.7.h_ref = s32[2048,1]{1,0:T(8,128)} copy(s32[2048,1]{0,1:T(1,128)} %bitcast.8) | data formatting | bytes 16384 | tf_op jit(solution)/shard_map/reshape | solution.py:206
  2.7 23.3 %heavy_sums.1 = f32[2048,128]{1,0:T(8,128)} custom-call(s32[2048,1]{1,0:T(8,128)} %copy.7.h_ref, s32[64,128]{1,0:T(8,128)} %bitcast.6, f32[8192,128]{1,0:T(8,128)} %v_ref.1), custom_call_target="tpu_custom_call" | custom-call | flops 8589934592 | bytes 4194304 | tf_op jit(solution)/shard_map/heavy_sums/pallas_call | solution.py:188
  26.0 12.5 %all-to-all-start.1 = ((f32[64,32,128]{2,1,0:T(8,128)}), f32[64,32,128]{2,1,0:T(8,128)S(1)}, u32[]{:S(2)}, u32[]{:S(2)}) async-start(f32[64,32,128]{2,1,0:T(8,128)} %bitcast.5), calls=%async_computation.1 | async-start | bytes 2097152 | tf_op jit(solution)/shard_map/all_to_all | solution.py:216
  38.5 5.3 %pack_blocks.1 = f32[2,4160,128]{2,1,0:T(8,128)} custom-call(s32[1,64]{1,0:T(1,128)} %off_ref.1, s32[1,64]{1,0:T(1,128)} %cnt_ref.1, s32[64,128]{1,0:T(8,128)} %bitcast.7, f32[8192,128]{1,0:T(8,128)} %v_ref.1), custom_call_target="tpu_custom_call" | custom-call | tf_op jit(solution)/shard_map/pack_blocks/pallas_call | solution.py:56
  43.8 14.1 %all-to-all-done.1 = f32[64,32,128]{2,1,0:T(8,128)S(1)} async-done(((f32[64,32,128]{2,1,0:T(8,128)}), f32[64,32,128]{2,1,0:T(8,128)S(1)}, u32[]{:S(2)}, u32[]{:S(2)}) %all-to-all-start.1) | async-done | bytes 1048608 | tf_op jit(solution)/shard_map/all_to_all | solution.py:216
  57.9 4.8 %all-to-all-start = ((f32[128,65,1,128]{3,2,1,0:T(1,128)}), f32[128,65,1,128]{3,2,1,0:T(1,128)}, u32[]{:S(2)}, u32[]{:S(2)}) async-start(f32[128,65,1,128]{3,2,1,0:T(1,128)} %bitcast.4), calls=%async_computation | async-start | bytes 8519680 | tf_op jit(solution)/shard_map/all_to_all | solution.py:213
  62.7 0.1 reduce_sum.9
  62.8 1.5 %collective-permute-start = (f32[32,128]{1,0:T(8,128)S(1)}, f32[32,128]{1,0:T(8,128)S(1)}, u32[]{:S(2)}, u32[]{:S(2)}) collective-permute-start(f32[32,128]{1,0:T(8,128)S(1)} %reduce_sum.9), channel_id=1, source_target_pairs={{0,64},{64,0},{1,65},{65,1},{2,66},{66,2},{3,67},{67,3},{4,68},{68... | collective-permute-start | bytes 49160 | tf_op jit(solution)/shard_map/ppermute | solution.py:220
  64.3 47.9 %collective-permute-done = f32[32,128]{1,0:T(8,128)S(1)} collective-permute-done((f32[32,128]{1,0:T(8,128)S(1)}, f32[32,128]{1,0:T(8,128)S(1)}, u32[]{:S(2)}, u32[]{:S(2)}) %collective-permute-start) | collective-permute-done | bytes 16416 | tf_op jit(solution)/shard_map/ppermute | solution.py:220
  112.2 0.6 add.3
  112.8 4.6 %all-to-all-done.recv_ref = f32[128,65,1,128]{3,2,1,0:T(1,128)} async-done(((f32[128,65,1,128]{3,2,1,0:T(1,128)}), f32[128,65,1,128]{3,2,1,0:T(1,128)}, u32[]{:S(2)}, u32[]{:S(2)}) %all-to-all-start) | async-done | bytes 4259872 | tf_op jit(solution)/shard_map/all_to_all | solution.py:213
  117.4 12.3 %light_sums.1 = f32[4096,128]{1,0:T(8,128)} custom-call(f32[128,65,1,128]{3,2,1,0:T(1,128)} %all-to-all-done.recv_ref), custom_call_target="tpu_custom_call" | custom-call | tf_op jit(solution)/shard_map/light_sums/pallas_call | solution.py:128
Async XLA Ops:
  26.0 31.9 %all-to-all-start.1 = ((f32[64,32,128]{2,1,0:T(8,128)}), f32[64,32,128]{2,1,0:T(8,128)S(1)}, u32[]{:S(2)}, u32[]{:S(2)}) async-start(f32[64,32,128]{2,1,0:T(8,128)} %bitcast.5), calls=%async_computation.1 | async-start | bytes 2097152 | tf_op jit(solution)/shard_map/all_to_all | solution.py:216
  57.9 59.5 %all-to-all-start = ((f32[128,65,1,128]{3,2,1,0:T(1,128)}), f32[128,65,1,128]{3,2,1,0:T(1,128)}, u32[]{:S(2)}, u32[]{:S(2)}) async-start(f32[128,65,1,128]{3,2,1,0:T(1,128)} %bitcast.4), calls=%async_computation | async-start | bytes 8519680 | tf_op jit(solution)/shard_map/all_to_all | solution.py:213
  62.8 49.4 %collective-permute-start = (f32[32,128]{1,0:T(8,128)S(1)}, f32[32,128]{1,0:T(8,128)S(1)}, u32[]{:S(2)}, u32[]{:S(2)}) collective-permute-start(f32[32,128]{1,0:T(8,128)S(1)} %reduce_sum.9), channel_id=1, source_target_pairs={{0,64},{64,0},{1,65},{65,1},{2,66},{66,2},{3,67},{67,3},{4,68},{68... | collective-permute-start | bytes 49160 | tf_op jit(solution)/shard_map/ppermute | solution.py:220

commit v2 on v1

--- a/solution.py
+++ b/solution.py
@@ -145,95 +145,128 @@
     )(recv)
 
 
-def heavy_kernel(values, keys, heavy_ids):
+def heavy_kernel(values, keys, heavy_ids, place):
     events, width = values.shape
     heavy = heavy_ids.shape[0]
+    tile = heavy // 2
     step_events = 2048
-    tile = 512
+    event_rows = events // LANES
     rows = step_events // LANES
-    steps = events // step_events
-
-    def body(h_ref, k_ref, v_ref, out_ref, ids, acc):
+    nx, nz, ny, nc = 4, 4, 2, 2
+    piece = heavy // (nx * nz * ny * nc)
+
+    def body(at_ref, h_ref, k_ref, v_ref, near_ref, far_ref, ids, rhs):
         c = pl.program_id(0)
 
         @pl.when(c == 0)
         def _():
-            ids[...] = jnp.broadcast_to(h_ref[...], ids.shape)
-
-        v = v_ref[...]
-        high = v.astype(jnp.bfloat16)
-        low = (v - high.astype(jnp.float32)).astype(jnp.bfloat16)
-        rhs = jnp.concatenate([high, low], axis=1)
-        key_rows = [k_ref[pl.ds(c * rows + j, 1), :] for j in range(rows)]
-        for t in range(heavy // tile):
-            span = pl.ds(t * tile, tile)
-            h = ids[span, :]
+            for p in range(nx * nz * ny * nc):
+                dc, dx, dz, dy = p // 32, (p // 8) % 4, (p // 2) % 4, p % 2
+                x = (at_ref[0] + dx) % nx
+                z = (at_ref[1] + dz) % nz
+                y = (at_ref[2] + dy) % ny
+                core = (at_ref[3] + dc) % nc
+                source = ((x * nz + z) * ny + y) * nc + core
+                column = h_ref[pl.ds(pl.multiple_of(source * piece, piece), piece), :]
+                ids[pl.ds(p * piece, piece), :] = jnp.broadcast_to(column, (piece, LANES))
+
+            def split(i, carry):
+                span = pl.ds(i * 512, 512)
+                v = v_ref[span, :]
+                high = v.astype(jnp.bfloat16)
+                rhs[span, :width] = high
+                rhs[span, width:] = (v - high.astype(jnp.float32)).astype(jnp.bfloat16)
+                return carry
+
+            lax.fori_loop(0, events // 512, split, 0)
+
+        h = ids[pl.ds(c * tile, tile), :]
+        total = None
+        for q in range(events // step_events):
             onehot = jnp.concatenate(
-                [jnp.where(h == row, 1.0, 0.0).astype(jnp.bfloat16) for row in key_rows], axis=1
+                [
+                    jnp.where(h == k_ref[pl.ds(q * rows + j, 1), :], 1.0, 0.0).astype(jnp.bfloat16)
+                    for j in range(rows)
+                ],
+                axis=1,
             )
-            added = jnp.dot(onehot, rhs, preferred_element_type=jnp.float32)
-
-            @pl.when(c == 0)
-            def _():
-                acc[span, :] = added
-
-            @pl.when(c != 0)
-            def _():
-                acc[span, :] += added
-
-        @pl.when(c == steps - 1)
+            added = jnp.dot(
+                onehot,
+                rhs[pl.ds(q * step_events, step_events), :],
+                preferred_element_type=jnp.float32,
+            )
+            total = added if total is None else total + added
+
+        @pl.when(c == 0)
         def _():
-            out_ref[...] = acc[:, :width] + acc[:, width:]
-
+            near_ref[...] = total[:, :width] + total[:, width:]
+
+        @pl.when(c == 1)
+        def _():
+            far_ref[...] = total[:, :width] + total[:, width:]
+
+    half = jax.ShapeDtypeStruct((tile, width), jnp.float32)
     return pl.pallas_call(
         body,
-        grid=(steps,),
-        out_shape=jax.ShapeDtypeStruct((heavy, width), jnp.float32),
+        grid=(2,),
+        out_shape=(half, half),
         in_specs=[
+            pl.BlockSpec(memory_space=pltpu.SMEM),
             pl.BlockSpec((heavy, 1), lambda c: (0, 0)),
-            pl.BlockSpec((events // LANES, LANES), lambda c: (0, 0)),
-            pl.BlockSpec((step_events, width), lambda c: (c, 0)),
-        ],
-        out_specs=pl.BlockSpec((heavy, width), lambda c: (0, 0)),
+            pl.BlockSpec((event_rows, LANES), lambda c: (0, 0)),
+            pl.BlockSpec((events, width), lambda c: (0, 0)),
+        ],
+        out_specs=(
+            pl.BlockSpec((tile, width), lambda c: (0, 0)),
+            pl.BlockSpec((tile, width), lambda c: (0, 0)),
+        ),
         scratch_shapes=[
             pltpu.VMEM((heavy, LANES), jnp.int32),
-            pltpu.VMEM((heavy, 2 * width), jnp.float32),
-        ],
-        cost_estimate=pl.CostEstimate(
-            flops=4 * events * heavy * width, bytes_accessed=4 * events * width, transcendentals=0
-        ),
+            pltpu.VMEM((events, 2 * width), jnp.bfloat16),
+        ],
         name="heavy_sums",
-    )(heavy_ids.reshape(heavy, 1), keys.reshape(events // LANES, LANES), values)
+    )(place, heavy_ids.reshape(heavy, 1), keys.reshape(event_rows, LANES), values)
+
+
+def ring_sum(x, axis):
+    size = x.shape[0]
+    total = x[0]
+    for d in range(1, size):
+        total = total + lax.ppermute(x[d], axis, [(i, (i + d) % size) for i in range(size)])
+    return total
 
 
 def per_device(values, key_ids, heavy_ids, block_offsets, block_counts):
-    owners = lax.axis_size("own")
+    own = ("x", "z", "y_hi", "core")
+    owners = lax.axis_size(own)
     pairs = lax.axis_size("rep")
+    place = jnp.stack([lax.axis_index(axis) for axis in own]).astype(jnp.int32)
     packed = pack_blocks(block_offsets, block_counts, key_ids, values, owners, pairs)
-    recv = lax.all_to_all(packed, ("rep", "own"), split_axis=0, concat_axis=0, tiled=True)
-    partial = heavy_kernel(values, key_ids, heavy_ids)
-    heavy, width = partial.shape
-    pieces = lax.all_to_all(
-        partial.reshape(owners, heavy // owners, width), "own", 0, 0, tiled=True
-    )
-    mine = jnp.sum(pieces, axis=0)
-    heavy_sums = mine + lax.ppermute(mine, "rep", [(0, 1), (1, 0)])
+    recv = lax.all_to_all(packed, ("rep",) + own, split_axis=0, concat_axis=0, tiled=True)
+    near, far = heavy_kernel(values, key_ids, heavy_ids, place)
+    width = near.shape[1]
+    near = near + lax.ppermute(far, "core", [(0, 1), (1, 0)])
+    near = ring_sum(near.reshape(4, -1, width), "x")
+    near = ring_sum(near.reshape(4, -1, width), "z")
+    keep, give = jnp.split(near, 2, axis=0)
+    column = ("rep", "y_hi")
+    near_rep = keep + lax.ppermute(give, column, [(0, 1), (1, 0), (2, 3), (3, 2)])
+    other_rep = lax.ppermute(keep, column, [(0, 2), (2, 0), (1, 3), (3, 1)])
+    other_rep = other_rep + lax.ppermute(give, column, [(0, 3), (3, 0), (1, 2), (2, 1)])
+    heavy_sums = near_rep + other_rep
     light_sums = light_kernel(recv)
     return (light_sums, heavy_sums)
 
 
 def solution(mesh):
-    placed = (
-        P(("rep", "own"), None),
-        P(("rep", "own")),
-        P(),
-        P(("rep", "own"), None),
-        P(("rep", "own"), None),
-    )
+    own = ("x", "z", "y_hi", "core")
+    every = ("rep",) + own
+    mesh = jax.sharding.Mesh(mesh.devices.reshape(2, 4, 4, 2, 2), every)
+    placed = (P(every, None), P(every), P(), P(every, None), P(every, None))
     return jax.shard_map(
         per_device,
         mesh=mesh,
         in_specs=placed,
-        out_specs=(P("own", None), P("own", None)),
+        out_specs=(P(own, None), P(own, None)),
         check_vma=False,
     )

time: 131 us -> 104 us (0.79)
  the two profiles are of different devices: /device:TPU:1 before, /device:TPU:6 now
where the time goes in v2:
time: 104 us
  waiting for transfers between devices  40.6 us (39%)
  Pallas kernels  31.7 us (30%)
  starting transfers between devices  27.2 us (26%)
  other arithmetic  2.38 us (2%)
  local copies, waits for them, and re-layouts  1.39 us (1%)
    ppermute x6, waiting for transfers between devices, ring_sum(): lax.ppermute(x[d], axis, [(i, (i + d) % size) for i in range(size)])  33.4 us
    pallas_call x1, Pallas kernels, heavy_kernel(): pl.pallas_call(body, grid=(2,), out_shape=(half, half), in_specs=[pl.Bloc...  13.9 us
    pallas_call x1, Pallas kernels, light_kernel(): pl.pallas_call(body, out_shape=jax.ShapeDtypeStruct((KEYS_DEV, width), jn...  12.4 us
    ppermute x6, starting transfers between devices, ring_sum(): lax.ppermute(x[d], axis, [(i, (i + d) % size) for i in range(size)])  11.6 us
    all_to_all x1, starting transfers between devices, per_device(): lax.all_to_all(packed, ('rep',) + own, split_axis=0, concat_axis=0, tiled...  10.9 us
    pallas_call x1, Pallas kernels, pack_blocks(): pl.pallas_call(body, out_shape=jax.ShapeDtypeStruct((reps, owners * block...  5.38 us
    ppermute x1, waiting for transfers between devices, per_device(): lax.ppermute(give, column, [(0, 3), (3, 0), (1, 2), (2, 1)])  2.79 us
    ppermute x1, starting transfers between devices, per_device(): other_rep = lax.ppermute(keep, column, [(0, 2), (2, 0), (1, 3), (3, 1)])  2.43 us
  transfers between devices with their start and end apart: 11, of which 7 were waited for; matrix products, arithmetic and copies ran while one was open for 4% of the time, Pallas kernels for 13%

profile of v2, /device:TPU:6, one launch (start us, length us, event | category | flops | bytes accessed | tf_op | source)
XLA Modules:
  0.0 103.9 jit_solution(4971667328094904892)
XLA Ops:
  0.6 5.4 %pack_blocks.1 = f32[2,4160,128]{2,1,0:T(8,128)} custom-call(s32[1,64]{1,0:T(1,128)} %off_ref.1, s32[1,64]{1,0:T(1,128)} %cnt_ref.1, s32[64,128]{1,0:T(8,128)} %bitcast.8, f32[8192,128]{1,0:T(8,128)} %v_ref.1), custom_call_target="tpu_custom_call" | custom-call | tf_op jit(solution)/shard_map/pack_blocks/pallas_call | solution.py:56
  6.0 0.0 copy-start
  6.0 10.9 %all-to-all-start = ((f32[128,65,1,128]{3,2,1,0:T(1,128)}), f32[128,65,1,128]{3,2,1,0:T(1,128)}, u32[]{:S(2)}, u32[]{:S(2)}) async-start(f32[128,65,1,128]{3,2,1,0:T(1,128)} %bitcast.7), calls=%async_computation | async-start | bytes 8519680 | tf_op jit(solution)/shard_map/all_to_all | solution.py:245
  16.9 0.0 copy-done
  16.9 1.3 %copy.7.h_ref = s32[2048,1]{1,0:T(8,128)} copy(s32[2048,1]{0,1:T(1,128)S(1)} %bitcast.10) | data formatting | bytes 16384 | tf_op jit(solution)/shard_map/reshape | solution.py:228
  18.3 0.6 pad_add_fusion.at_ref
  18.9 13.9 %heavy_sums.1 = (f32[1024,128]{1,0:T(8,128)}, f32[1024,128]{1,0:T(8,128)}) custom-call(s32[4]{0:T(128)} %pad_add_fusion.at_ref, s32[2048,1]{1,0:T(8,128)} %copy.7.h_ref, s32[64,128]{1,0:T(8,128)} %bitcast.9, f32[8192,128]{1,0:T(8,128)} %v_ref.1), custom_call_target="tpu_custom_call" | custom-call | tf_op jit(solution)/shard_map/heavy_sums/pallas_call | solution.py:209
  32.8 0.1 collective-permute-start
  32.9 2.0 %collective-permute-done = f32[1024,128]{1,0:T(8,128)S(1)} collective-permute-done((f32[1024,128]{1,0:T(8,128)}, f32[1024,128]{1,0:T(8,128)S(1)}, u32[]{:S(2)}, u32[]{:S(2)}) %collective-permute-start) | collective-permute-done | bytes 524320 | tf_op jit(solution)/shard_map/ppermute | solution.py:248
  34.9 1.1 %add.30 = f32[1024,128]{1,0:T(8,128)S(1)} add(f32[1024,128]{1,0:T(8,128)} %get-tuple-element.4, f32[1024,128]{1,0:T(8,128)S(1)} %collective-permute-done) | non-fusion elementwise | flops 131072 | bytes 1572864 | tf_op jit(solution)/shard_map/add | solution.py:248
  36.0 0.9 collective-permute-start.3
  37.0 1.7 %collective-permute-start.2 = (f32[256,128]{1,0:T(8,128)S(1)}, f32[256,128]{1,0:T(8,128)S(1)}, u32[]{:S(2)}, u32[]{:S(2)}) collective-permute-start(f32[256,128]{1,0:T(8,128)S(1)} %get-tuple-element.8), channel_id=1, source_target_pairs={{0,32},{16,48},{32,0},{48,16},{1,33},{17,49},{33,1},{49,17},{2,34}... | collective-permute-start | bytes 393224 | tf_op jit(solution)/shard_map/ppermute | solution.py:235
  38.7 1.5 %collective-permute-start.1 = (f32[256,128]{1,0:T(8,128)S(1)}, f32[256,128]{1,0:T(8,128)S(1)}, u32[]{:S(2)}, u32[]{:S(2)}) collective-permute-start(f32[256,128]{1,0:T(8,128)S(1)} %get-tuple-element.6), channel_id=1, source_target_pairs={{0,16},{16,32},{32,48},{48,0},{1,17},{17,33},{33,49},{49,1},{2,18}... | collective-permute-start | bytes 393224 | tf_op jit(solution)/shard_map/ppermute | solution.py:235
  40.2 25.7 %collective-permute-done.3 = f32[256,128]{1,0:T(8,128)S(1)} collective-permute-done((f32[256,128]{1,0:T(8,128)S(1)}, f32[256,128]{1,0:T(8,128)S(1)}, u32[]{:S(2)}, u32[]{:S(2)}) %collective-permute-start.3) | collective-permute-done | bytes 131104 | tf_op jit(solution)/shard_map/ppermute | solution.py:235
  65.9 3.9 %collective-permute-done.2 = f32[256,128]{1,0:T(8,128)S(1)} collective-permute-done((f32[256,128]{1,0:T(8,128)S(1)}, f32[256,128]{1,0:T(8,128)S(1)}, u32[]{:S(2)}, u32[]{:S(2)}) %collective-permute-start.2) | collective-permute-done | bytes 131104 | tf_op jit(solution)/shard_map/ppermute | solution.py:235
  69.8 0.0 collective-permute-done.1
  69.9 3.3 %collective-permute-start.6 = (f32[64,128]{1,0:T(8,128)S(1)}, f32[64,128]{1,0:T(8,128)S(1)}, u32[]{:S(2)}, u32[]{:S(2)}) collective-permute-start(f32[64,128]{1,0:T(8,128)S(1)} %get-tuple-element.10), channel_id=1, source_target_pairs={{0,12},{4,0},{8,4},{12,8},{1,13},{5,1},{9,5},{13,9},{2,14},{6,2},{... | collective-permute-start | bytes 98312 | tf_op jit(solution)/shard_map/ppermute | solution.py:235
  73.1 2.8 %collective-permute-start.5 = (f32[64,128]{1,0:T(8,128)S(1)}, f32[64,128]{1,0:T(8,128)S(1)}, u32[]{:S(2)}, u32[]{:S(2)}) collective-permute-start(f32[64,128]{1,0:T(8,128)S(1)} %get-tuple-element.11), channel_id=1, source_target_pairs={{0,8},{4,12},{8,0},{12,4},{1,9},{5,13},{9,1},{13,5},{2,10},{6,14},... | collective-permute-start | bytes 98312 | tf_op jit(solution)/shard_map/ppermute | solution.py:235
  76.0 1.3 %collective-permute-start.4 = (f32[64,128]{1,0:T(8,128)S(1)}, f32[64,128]{1,0:T(8,128)S(1)}, u32[]{:S(2)}, u32[]{:S(2)}) collective-permute-start(f32[64,128]{1,0:T(8,128)S(1)} %get-tuple-element.9), channel_id=1, source_target_pairs={{0,4},{4,8},{8,12},{12,0},{1,5},{5,9},{9,13},{13,1},{2,6},{6,10},{... | collective-permute-start | bytes 98312 | tf_op jit(solution)/shard_map/ppermute | solution.py:235
  77.3 0.0 collective-permute-done.6
  77.3 1.2 %collective-permute-done.5 = f32[64,128]{1,0:T(8,128)S(1)} collective-permute-done((f32[64,128]{1,0:T(8,128)S(1)}, f32[64,128]{1,0:T(8,128)S(1)}, u32[]{:S(2)}, u32[]{:S(2)}) %collective-permute-start.5) | collective-permute-done | bytes 32800 | tf_op jit(solution)/shard_map/ppermute | solution.py:235
  78.6 2.5 %collective-permute-done.4 = f32[64,128]{1,0:T(8,128)S(1)} collective-permute-done((f32[64,128]{1,0:T(8,128)S(1)}, f32[64,128]{1,0:T(8,128)S(1)}, u32[]{:S(2)}, u32[]{:S(2)}) %collective-permute-start.4) | collective-permute-done | bytes 32800 | tf_op jit(solution)/shard_map/ppermute | solution.py:235
  81.1 2.4 %collective-permute-start.8 = (f32[32,128]{1,0:T(8,128)S(1)}, f32[32,128]{1,0:T(8,128)S(1)}, u32[]{:S(2)}, u32[]{:S(2)}) collective-permute-start(f32[32,128]{1,0:T(8,128)S(1)} %get-tuple-element.13), channel_id=1, source_target_pairs={{0,64},{64,0},{2,66},{66,2},{1,65},{65,1},{3,67},{67,3},{4,68},{68... | collective-permute-start | bytes 49160 | tf_op jit(solution)/shard_map/ppermute | solution.py:254
  83.6 2.1 %collective-permute-start.9 = (f32[32,128]{1,0:T(8,128)S(1)}, f32[32,128]{1,0:T(8,128)S(1)}, u32[]{:S(2)}, u32[]{:S(2)}) collective-permute-start(f32[32,128]{1,0:T(8,128)S(1)} %get-tuple-element.12), channel_id=1, source_target_pairs={{0,66},{66,0},{2,64},{64,2},{1,67},{67,1},{3,65},{65,3},{4,70},{70... | collective-permute-start | bytes 49160 | tf_op jit(solution)/shard_map/ppermute | solution.py:255
  85.6 0.1 collective-permute-start.7
  85.7 0.0 collective-permute-done.8
  85.7 2.8 %collective-permute-done.9 = f32[32,128]{1,0:T(8,128)S(1)} collective-permute-done((f32[32,128]{1,0:T(8,128)S(1)}, f32[32,128]{1,0:T(8,128)S(1)}, u32[]{:S(2)}, u32[]{:S(2)}) %collective-permute-start.9) | collective-permute-done | bytes 16416 | tf_op jit(solution)/shard_map/ppermute | solution.py:255
  88.5 2.4 %collective-permute-done.7 = f32[32,128]{1,0:T(8,128)S(1)} collective-permute-done((f32[32,128]{1,0:T(8,128)S(1)}, f32[32,128]{1,0:T(8,128)S(1)}, u32[]{:S(2)}, u32[]{:S(2)}) %collective-permute-start.7) | collective-permute-done | bytes 16416 | tf_op jit(solution)/shard_map/ppermute | solution.py:253
  90.9 0.6 add_add_fusion
  91.5 0.0 all-to-all-done.recv_ref
  91.5 12.4 %light_sums.1 = f32[4096,128]{1,0:T(8,128)} custom-call(f32[128,65,1,128]{3,2,1,0:T(1,128)} %all-to-all-done.recv_ref), custom_call_target="tpu_custom_call" | custom-call | tf_op jit(solution)/shard_map/light_sums/pallas_call | solution.py:128
  (5 shorter events, 0.1 us)
Async XLA Ops:
  6.0 10.9 %copy-start = (s32[2048]{0:T(1024)S(1)}, s32[2048]{0:T(1024)}, u32[]{:S(2)}) copy-start(s32[2048]{0:T(1024)} %param.7) | copy-start | bytes 24580
  6.0 85.5 %all-to-all-start = ((f32[128,65,1,128]{3,2,1,0:T(1,128)}), f32[128,65,1,128]{3,2,1,0:T(1,128)}, u32[]{:S(2)}, u32[]{:S(2)}) async-start(f32[128,65,1,128]{3,2,1,0:T(1,128)} %bitcast.7), calls=%async_computation | async-start | bytes 8519680 | tf_op jit(solution)/shard_map/all_to_all | solution.py:245
  32.8 2.1 %collective-permute-start = (f32[1024,128]{1,0:T(8,128)}, f32[1024,128]{1,0:T(8,128)S(1)}, u32[]{:S(2)}, u32[]{:S(2)}) collective-permute-start(f32[1024,128]{1,0:T(8,128)} %get-tuple-element.5), channel_id=1, source_target_pairs={{0,1},{1,0},{2,3},{3,2},{4,5},{5,4},{6,7},{7,6},{8,9},{9,8},{10,11... | collective-permute-start | bytes 1572872 | tf_op jit(solution)/shard_map/ppermute | solution.py:248
  36.0 29.9 %collective-permute-start.3 = (f32[256,128]{1,0:T(8,128)S(1)}, f32[256,128]{1,0:T(8,128)S(1)}, u32[]{:S(2)}, u32[]{:S(2)}) collective-permute-start(f32[256,128]{1,0:T(8,128)S(1)} %get-tuple-element.7), channel_id=1, source_target_pairs={{0,48},{16,0},{32,16},{48,32},{1,49},{17,1},{33,17},{49,33},{2,50}... | collective-permute-start | bytes 393224 | tf_op jit(solution)/shard_map/ppermute | solution.py:235
  37.0 32.9 %collective-permute-start.2 = (f32[256,128]{1,0:T(8,128)S(1)}, f32[256,128]{1,0:T(8,128)S(1)}, u32[]{:S(2)}, u32[]{:S(2)}) collective-permute-start(f32[256,128]{1,0:T(8,128)S(1)} %get-tuple-element.8), channel_id=1, source_target_pairs={{0,32},{16,48},{32,0},{48,16},{1,33},{17,49},{33,1},{49,17},{2,34}... | collective-permute-start | bytes 393224 | tf_op jit(solution)/shard_map/ppermute | solution.py:235
  38.7 31.1 %collective-permute-start.1 = (f32[256,128]{1,0:T(8,128)S(1)}, f32[256,128]{1,0:T(8,128)S(1)}, u32[]{:S(2)}, u32[]{:S(2)}) collective-permute-start(f32[256,128]{1,0:T(8,128)S(1)} %get-tuple-element.6), channel_id=1, source_target_pairs={{0,16},{16,32},{32,48},{48,0},{1,17},{17,33},{33,49},{49,1},{2,18}... | collective-permute-start | bytes 393224 | tf_op jit(solution)/shard_map/ppermute | solution.py:235
  69.9 7.4 %collective-permute-start.6 = (f32[64,128]{1,0:T(8,128)S(1)}, f32[64,128]{1,0:T(8,128)S(1)}, u32[]{:S(2)}, u32[]{:S(2)}) collective-permute-start(f32[64,128]{1,0:T(8,128)S(1)} %get-tuple-element.10), channel_id=1, source_target_pairs={{0,12},{4,0},{8,4},{12,8},{1,13},{5,1},{9,5},{13,9},{2,14},{6,2},{... | collective-permute-start | bytes 98312 | tf_op jit(solution)/shard_map/ppermute | solution.py:235
  73.1 5.4 %collective-permute-start.5 = (f32[64,128]{1,0:T(8,128)S(1)}, f32[64,128]{1,0:T(8,128)S(1)}, u32[]{:S(2)}, u32[]{:S(2)}) collective-permute-start(f32[64,128]{1,0:T(8,128)S(1)} %get-tuple-element.11), channel_id=1, source_target_pairs={{0,8},{4,12},{8,0},{12,4},{1,9},{5,13},{9,1},{13,5},{2,10},{6,14},... | collective-permute-start | bytes 98312 | tf_op jit(solution)/shard_map/ppermute | solution.py:235
  76.0 5.1 %collective-permute-start.4 = (f32[64,128]{1,0:T(8,128)S(1)}, f32[64,128]{1,0:T(8,128)S(1)}, u32[]{:S(2)}, u32[]{:S(2)}) collective-permute-start(f32[64,128]{1,0:T(8,128)S(1)} %get-tuple-element.9), channel_id=1, source_target_pairs={{0,4},{4,8},{8,12},{12,0},{1,5},{5,9},{9,13},{13,1},{2,6},{6,10},{... | collective-permute-start | bytes 98312 | tf_op jit(solution)/shard_map/ppermute | solution.py:235
  81.1 4.6 %collective-permute-start.8 = (f32[32,128]{1,0:T(8,128)S(1)}, f32[32,128]{1,0:T(8,128)S(1)}, u32[]{:S(2)}, u32[]{:S(2)}) collective-permute-start(f32[32,128]{1,0:T(8,128)S(1)} %get-tuple-element.13), channel_id=1, source_target_pairs={{0,64},{64,0},{2,66},{66,2},{1,65},{65,1},{3,67},{67,3},{4,68},{68... | collective-permute-start | bytes 49160 | tf_op jit(solution)/shard_map/ppermute | solution.py:254
  83.6 4.9 %collective-permute-start.9 = (f32[32,128]{1,0:T(8,128)S(1)}, f32[32,128]{1,0:T(8,128)S(1)}, u32[]{:S(2)}, u32[]{:S(2)}) collective-permute-start(f32[32,128]{1,0:T(8,128)S(1)} %get-tuple-element.12), channel_id=1, source_target_pairs={{0,66},{66,0},{2,64},{64,2},{1,67},{67,1},{3,65},{65,3},{4,70},{70... | collective-permute-start | bytes 49160 | tf_op jit(solution)/shard_map/ppermute | solution.py:255
  85.6 5.2 %collective-permute-start.7 = (f32[32,128]{1,0:T(8,128)S(1)}, f32[32,128]{1,0:T(8,128)S(1)}, u32[]{:S(2)}, u32[]{:S(2)}) collective-permute-start(f32[32,128]{1,0:T(8,128)S(1)} %get-tuple-element.12), channel_id=1, source_target_pairs={{0,2},{2,0},{64,66},{66,64},{1,3},{3,1},{65,67},{67,65},{4,6},{6,4... | collective-permute-start | bytes 49160 | tf_op jit(solution)/shard_map/ppermute | solution.py:253

commit v3 on v2

--- a/solution.py
+++ b/solution.py
@@ -12,17 +12,27 @@
 CHUNK = 32
 
 
-def pack_blocks(offs, cnts, keys, values, owners, reps):
+def pack_blocks(offs, cnts, keys, values, sizes):
+    nr, nx, nz, ny, nc = sizes
     events, width = values.shape
     key_rows = events // LANES
     block = CAP + 1
-
-    def body(off_ref, cnt_ref, keys_ref, val_ref, out_ref, buf, krow, arow, sem):
+    groups, members = nz * ny, nx * nc
+    owners = groups * members
+
+    def owner_of(g, m):
+        return (((m // nc) * nz + g // ny) * ny + g % ny) * nc + m % nc
+
+    def body(off_ref, cnt_ref, keys_ref, val_ref, out_ref, rows, buf, krow, arow, in_sem, out_sem):
         lane = lax.broadcasted_iota(jnp.int32, (1, LANES), 1)
 
-        def step(o, carry):
+        load = pltpu.make_async_copy(val_ref, rows, in_sem)
+        load.start()
+
+        def block_keys(b, carry):
+            o = owner_of(b // members, b % members)
             off = off_ref[0, o]
-            cnt = cnt_ref[0, o]
+            end = off + cnt_ref[0, o]
             start = jnp.minimum(off, events - CAP)
             row = start // LANES
             shift = start - row * LANES
@@ -30,43 +40,58 @@
             first = lane >= shift
             pos = jnp.where(first, row * LANES + lane, (row + 1) * LANES + lane)
             key = jnp.where(first, keys_ref[pl.ds(row, 1), :], keys_ref[pl.ds(row_next, 1), :])
-            inside = (pos >= off) & (pos < off + cnt)
-            krow[pl.ds(o, 1), :] = jnp.where(inside, key - o * KEYS_DEV, KEYS_DEV)
-            arow[pl.ds(o, 1), :] = jnp.full((1, LANES), shift, jnp.int32)
-            buf[pl.ds(o * block, CAP), :] = val_ref[pl.ds(start, CAP), :]
-            return carry
-
-        lax.fori_loop(0, owners, step, 0, unroll=8)
+            inside = (pos >= off) & (pos < end)
+            krow[pl.ds(b, 1), :] = jnp.where(inside, key - o * KEYS_DEV, KEYS_DEV)
+            arow[pl.ds(b, 1), :] = jnp.full((1, LANES), shift, jnp.int32)
+            return carry
+
+        lax.fori_loop(0, owners, block_keys, 0, unroll=16)
         rolled = krow[...]
         shifts = arow[...]
         for bit in range(7):
             moved = pltpu.roll(rolled, LANES - (1 << bit), 1)
             rolled = jnp.where((shifts >> bit) & 1 == 1, moved, rolled)
         krow[...] = rolled
-        for o in range(owners):
-            buf[pl.ds(o * block + CAP, 1), :] = krow[pl.ds(o, 1), :].astype(jnp.float32)
-        copies = [pltpu.make_async_copy(buf, out_ref.at[r], sem.at[r]) for r in range(reps)]
-        for copy in copies:
-            copy.start()
-        for copy in copies:
-            copy.wait()
+        load.wait()
+        stores = []
+        for g in range(groups):
+            for m in range(members):
+                b = g * members + m
+                start = jnp.minimum(off_ref[0, owner_of(g, m)], events - CAP)
+                buf[pl.ds(b * block, CAP), :] = rows[pl.ds(start, CAP), :]
+                buf[pl.ds(b * block + CAP, 1), :] = krow[pl.ds(b, 1), :].astype(jnp.float32)
+            span = pl.ds(g * members * block, members * block)
+            for r in range(nr):
+                store = pltpu.make_async_copy(
+                    buf.at[span], out_ref.at[g * nr + r], out_sem.at[g * nr + r]
+                )
+                store.start()
+                stores.append(store)
+        for store in stores:
+            store.wait()
 
     smem = pl.BlockSpec(memory_space=pltpu.SMEM)
-    vmem = pl.BlockSpec(memory_space=pltpu.VMEM)
     packed = pl.pallas_call(
         body,
-        out_shape=jax.ShapeDtypeStruct((reps, owners * block, width), jnp.float32),
-        in_specs=[smem, smem, vmem, vmem],
+        out_shape=jax.ShapeDtypeStruct((groups * nr, members * block, width), jnp.float32),
+        in_specs=[
+            smem,
+            smem,
+            pl.BlockSpec(memory_space=pltpu.VMEM),
+            pl.BlockSpec(memory_space=pl.ANY),
+        ],
         out_specs=pl.BlockSpec(memory_space=pl.ANY),
         scratch_shapes=[
+            pltpu.VMEM((events, width), jnp.float32),
             pltpu.VMEM((owners * block, width), jnp.float32),
             pltpu.VMEM((owners, LANES), jnp.int32),
             pltpu.VMEM((owners, LANES), jnp.int32),
-            pltpu.SemaphoreType.DMA((reps,)),
+            pltpu.SemaphoreType.DMA,
+            pltpu.SemaphoreType.DMA((groups * nr,)),
         ],
         name="pack_blocks",
     )(offs, cnts, keys.reshape(key_rows, LANES), values)
-    return packed.reshape(reps * owners, block, 1, width)
+    return packed.reshape(nr * owners, block, 1, width)
 
 
 def light_kernel(recv):
@@ -75,7 +100,7 @@
 
     def body(recv_ref, out_ref, rows, kint, ksm, *rest):
         acc = rest[:BANKS]
-        key_sem, smem_sem, row_sems = rest[BANKS:]
+        key_sem, smem_sem, row_sems, out_sems = rest[BANKS:]
         key_copy = pltpu.make_async_copy(recv_ref.at[:, CAP], rows.at[:, CAP], key_sem)
         key_copy.start()
         copies = []
@@ -120,16 +145,25 @@
             total = acc[0][span, :]
             for bank in acc[1:]:
                 total = total + bank[span, :]
-            out_ref[span, :] = total
-            return carry
-
-        lax.fori_loop(0, KEYS_DEV // 64, finish, 0)
+            acc[0][span, :] = total
+            return carry
+
+        parts = 8
+        stores = []
+        for c in range(parts):
+            step = KEYS_DEV // parts
+            lax.fori_loop(c * step // 64, (c + 1) * step // 64, finish, 0)
+            span = pl.ds(c * step, step)
+            stores.append(pltpu.make_async_copy(acc[0].at[span], out_ref.at[span], out_sems.at[c]))
+            stores[c].start()
+        for store in stores:
+            store.wait()
 
     return pl.pallas_call(
         body,
         out_shape=jax.ShapeDtypeStruct((KEYS_DEV, width), jnp.float32),
         in_specs=[pl.BlockSpec(memory_space=pl.ANY)],
-        out_specs=pl.BlockSpec(memory_space=pltpu.VMEM),
+        out_specs=pl.BlockSpec(memory_space=pl.ANY),
         scratch_shapes=[
             pltpu.VMEM((senders, block, 1, width), jnp.float32),
             pltpu.VMEM((senders, 1, width), jnp.int32),
@@ -140,33 +174,29 @@
             pltpu.SemaphoreType.DMA,
             pltpu.SemaphoreType.DMA,
             pltpu.SemaphoreType.DMA((chunks,)),
+            pltpu.SemaphoreType.DMA((8,)),
         ],
         name="light_sums",
     )(recv)
 
 
-def heavy_kernel(values, keys, heavy_ids, place):
+def heavy_kernel(values, keys, heavy_ids, core, owners):
     events, width = values.shape
     heavy = heavy_ids.shape[0]
     tile = heavy // 2
     step_events = 2048
     event_rows = events // LANES
     rows = step_events // LANES
-    nx, nz, ny, nc = 4, 4, 2, 2
-    piece = heavy // (nx * nz * ny * nc)
-
-    def body(at_ref, h_ref, k_ref, v_ref, near_ref, far_ref, ids, rhs):
+    half = owners // 2
+    piece = heavy // owners
+
+    def body(core_ref, h_ref, k_ref, v_ref, near_ref, far_ref, ids, rhs):
         c = pl.program_id(0)
 
         @pl.when(c == 0)
         def _():
-            for p in range(nx * nz * ny * nc):
-                dc, dx, dz, dy = p // 32, (p // 8) % 4, (p // 2) % 4, p % 2
-                x = (at_ref[0] + dx) % nx
-                z = (at_ref[1] + dz) % nz
-                y = (at_ref[2] + dy) % ny
-                core = (at_ref[3] + dc) % nc
-                source = ((x * nz + z) * ny + y) * nc + core
+            for p in range(owners):
+                source = (p % half) * 2 + (core_ref[0] + p // half) % 2
                 column = h_ref[pl.ds(pl.multiple_of(source * piece, piece), piece), :]
                 ids[pl.ds(p * piece, piece), :] = jnp.broadcast_to(column, (piece, LANES))
 
@@ -205,11 +235,11 @@
         def _():
             far_ref[...] = total[:, :width] + total[:, width:]
 
-    half = jax.ShapeDtypeStruct((tile, width), jnp.float32)
+    side = jax.ShapeDtypeStruct((tile, width), jnp.float32)
     return pl.pallas_call(
         body,
         grid=(2,),
-        out_shape=(half, half),
+        out_shape=(side, side),
         in_specs=[
             pl.BlockSpec(memory_space=pltpu.SMEM),
             pl.BlockSpec((heavy, 1), lambda c: (0, 0)),
@@ -225,36 +255,24 @@
             pltpu.VMEM((events, 2 * width), jnp.bfloat16),
         ],
         name="heavy_sums",
-    )(place, heavy_ids.reshape(heavy, 1), keys.reshape(event_rows, LANES), values)
-
-
-def ring_sum(x, axis):
-    size = x.shape[0]
-    total = x[0]
-    for d in range(1, size):
-        total = total + lax.ppermute(x[d], axis, [(i, (i + d) % size) for i in range(size)])
-    return total
+    )(core, heavy_ids.reshape(heavy, 1), keys.reshape(event_rows, LANES), values)
 
 
 def per_device(values, key_ids, heavy_ids, block_offsets, block_counts):
     own = ("x", "z", "y_hi", "core")
+    sizes = tuple(lax.axis_size(axis) for axis in ("rep",) + own)
     owners = lax.axis_size(own)
-    pairs = lax.axis_size("rep")
-    place = jnp.stack([lax.axis_index(axis) for axis in own]).astype(jnp.int32)
-    packed = pack_blocks(block_offsets, block_counts, key_ids, values, owners, pairs)
-    recv = lax.all_to_all(packed, ("rep",) + own, split_axis=0, concat_axis=0, tiled=True)
-    near, far = heavy_kernel(values, key_ids, heavy_ids, place)
-    width = near.shape[1]
+    packed = pack_blocks(block_offsets, block_counts, key_ids, values, sizes)
+    order = ("z", "y_hi", "rep", "x", "core")
+    recv = lax.all_to_all(packed, order, split_axis=0, concat_axis=0, tiled=True)
+    core = lax.axis_index("core").astype(jnp.int32).reshape(1)
+    near, far = heavy_kernel(values, key_ids, heavy_ids, core, owners)
     near = near + lax.ppermute(far, "core", [(0, 1), (1, 0)])
-    near = ring_sum(near.reshape(4, -1, width), "x")
-    near = ring_sum(near.reshape(4, -1, width), "z")
-    keep, give = jnp.split(near, 2, axis=0)
-    column = ("rep", "y_hi")
-    near_rep = keep + lax.ppermute(give, column, [(0, 1), (1, 0), (2, 3), (3, 2)])
-    other_rep = lax.ppermute(keep, column, [(0, 2), (2, 0), (1, 3), (3, 1)])
-    other_rep = other_rep + lax.ppermute(give, column, [(0, 3), (3, 0), (1, 2), (2, 1)])
-    heavy_sums = near_rep + other_rep
+    pieces = near.reshape(owners // 2, -1, near.shape[1])
+    pieces = jnp.concatenate([pieces, pieces], axis=0)
+    pieces = lax.all_to_all(pieces, ("rep", "x", "z", "y_hi"), 0, 0, tiled=True)
     light_sums = light_kernel(recv)
+    heavy_sums = jnp.sum(pieces, axis=0)
     return (light_sums, heavy_sums)
 
 

time: 104 us -> 123 us (1.18)
  the two profiles are of different devices: /device:TPU:6 before, /device:TPU:1 now
where the time goes in v3:
time: 123 us; the launch traced here: 122 us
  waiting for transfers between devices  66.9 us (54%)
  Pallas kernels  30.6 us (25%)
  starting transfers between devices  19.2 us (16%)
  other arithmetic  2.92 us (2%)
  local copies, waits for them, and re-layouts  2.04 us (2%)
    all_to_all x1, waiting for transfers between devices, per_device(): lax.all_to_all(packed, order, split_axis=0, concat_axis=0, tiled=True)  52.8 us
    pallas_call x1, Pallas kernels, heavy_kernel(): pl.pallas_call(body, grid=(2,), out_shape=(side, side), in_specs=[pl.Bloc...  13.7 us
    all_to_all x1, waiting for transfers between devices, per_device(): pieces = lax.all_to_all(pieces, ('rep', 'x', 'z', 'y_hi'), 0, 0, tiled=True)  12.3 us
    pallas_call x1, Pallas kernels, light_kernel(): pl.pallas_call(body, out_shape=jax.ShapeDtypeStruct((KEYS_DEV, width), jn...  11.8 us
    all_to_all x1, starting transfers between devices, per_device(): pieces = lax.all_to_all(pieces, ('rep', 'x', 'z', 'y_hi'), 0, 0, tiled=True)  11.2 us
    all_to_all x1, starting transfers between devices, per_device(): lax.all_to_all(packed, order, split_axis=0, concat_axis=0, tiled=True)  6.56 us
    pallas_call x1, Pallas kernels, pack_blocks(): pl.pallas_call(body, out_shape=jax.ShapeDtypeStruct((groups * nr, members...  5.12 us
  transfers between devices with their start and end apart: 3, of which 3 were waited for; matrix products, arithmetic and copies ran while one was open for 1% of the time, Pallas kernels for 4%

profile of v3, /device:TPU:1, one launch (start us, length us, event | category | flops | bytes accessed | tf_op | source)
XLA Modules:
  0.0 122.3 jit_solution(9822730440045361462)
XLA Ops:
  0.6 2.0 %copy.7.h_ref = s32[2048,1]{1,0:T(8,128)} copy(s32[2048,1]{0,1:T(1,128)} %bitcast.9) | data formatting | bytes 16384 | tf_op jit(solution)/shard_map/reshape | solution.py:258
  2.7 13.7 %heavy_sums.1 = (f32[1024,128]{1,0:T(8,128)}, f32[1024,128]{1,0:T(8,128)}) custom-call(s32[1]{0:T(128)} %bitcast.2.core_ref, s32[2048,1]{1,0:T(8,128)} %copy.7.h_ref, s32[64,128]{1,0:T(8,128)} %bitcast.7, f32[8192,128]{1,0:T(8,128)} %v_ref.1), custom_call_target="tpu_custom_call" | custom-call | tf_op jit(solution)/shard_map/heavy_sums/pallas_call | solution.py:239
  16.4 1.4 %collective-permute-start = (f32[1024,128]{1,0:T(8,128)}, f32[1024,128]{1,0:T(8,128)S(1)}, u32[]{:S(2)}, u32[]{:S(2)}) collective-permute-start(f32[1024,128]{1,0:T(8,128)} %get-tuple-element.5), channel_id=1, source_target_pairs={{0,1},{1,0},{2,3},{3,2},{4,5},{5,4},{6,7},{7,6},{8,9},{9,8},{10,11... | collective-permute-start | bytes 1572872 | tf_op jit(solution)/shard_map/ppermute | solution.py:270
  17.8 1.7 %collective-permute-done = f32[1024,128]{1,0:T(8,128)S(1)} collective-permute-done((f32[1024,128]{1,0:T(8,128)}, f32[1024,128]{1,0:T(8,128)S(1)}, u32[]{:S(2)}, u32[]{:S(2)}) %collective-permute-start) | collective-permute-done | bytes 524320 | tf_op jit(solution)/shard_map/ppermute | solution.py:270
  19.5 1.1 add.3
  20.6 1.1 pad_maximum_fusion
  21.7 11.2 %all-to-all-start.1 = ((f32[64,32,128]{2,1,0:T(8,128)}), f32[64,32,128]{2,1,0:T(8,128)S(1)}, u32[]{:S(2)}, u32[]{:S(2)}) async-start(f32[64,32,128]{2,1,0:T(8,128)} %pad_maximum_fusion), calls=%async_computation.1 | async-start | bytes 2097152 | tf_op jit(solution)/shard_map/all_to_all | solution.py:273
  33.0 5.1 %pack_blocks.1 = f32[16,520,128]{2,1,0:T(8,128)} custom-call(s32[1,64]{1,0:T(1,128)} %off_ref.1, s32[1,64]{1,0:T(1,128)} %cnt_ref.1, s32[64,128]{1,0:T(8,128)} %bitcast.8, f32[8192,128]{1,0:T(8,128)} %v_ref.1), custom_call_target="tpu_custom_call" | custom-call | tf_op jit(solution)/shard_map/pack_blocks/pallas_call | solution.py:74
  38.1 12.3 %all-to-all-done.1 = f32[64,32,128]{2,1,0:T(8,128)S(1)} async-done(((f32[64,32,128]{2,1,0:T(8,128)}), f32[64,32,128]{2,1,0:T(8,128)S(1)}, u32[]{:S(2)}, u32[]{:S(2)}) %all-to-all-start.1) | async-done | bytes 1048608 | tf_op jit(solution)/shard_map/all_to_all | solution.py:273
  50.5 6.6 %all-to-all-start = ((f32[128,65,1,128]{3,2,1,0:T(1,128)}), f32[128,65,1,128]{3,2,1,0:T(1,128)}, u32[]{:S(2)}, u32[]{:S(2)}) async-start(f32[128,65,1,128]{3,2,1,0:T(1,128)} %bitcast.5), calls=%async_computation | async-start | bytes 8519680 | tf_op jit(solution)/shard_map/all_to_all | solution.py:267
  57.0 0.7 reduce_sum.9
  57.7 52.8 %all-to-all-done.recv_ref = f32[128,65,1,128]{3,2,1,0:T(1,128)} async-done(((f32[128,65,1,128]{3,2,1,0:T(1,128)}), f32[128,65,1,128]{3,2,1,0:T(1,128)}, u32[]{:S(2)}, u32[]{:S(2)}) %all-to-all-start) | async-done | bytes 4259872 | tf_op jit(solution)/shard_map/all_to_all | solution.py:267
  110.5 11.8 %light_sums.1 = f32[4096,128]{1,0:T(8,128)} custom-call(f32[128,65,1,128]{3,2,1,0:T(1,128)} %all-to-all-done.recv_ref), custom_call_target="tpu_custom_call" | custom-call | tf_op jit(solution)/shard_map/light_sums/pallas_call | solution.py:162
Async XLA Ops:
  16.4 3.1 %collective-permute-start = (f32[1024,128]{1,0:T(8,128)}, f32[1024,128]{1,0:T(8,128)S(1)}, u32[]{:S(2)}, u32[]{:S(2)}) collective-permute-start(f32[1024,128]{1,0:T(8,128)} %get-tuple-element.5), channel_id=1, source_target_pairs={{0,1},{1,0},{2,3},{3,2},{4,5},{5,4},{6,7},{7,6},{8,9},{9,8},{10,11... | collective-permute-start | bytes 1572872 | tf_op jit(solution)/shard_map/ppermute | solution.py:270
  21.7 28.7 %all-to-all-start.1 = ((f32[64,32,128]{2,1,0:T(8,128)}), f32[64,32,128]{2,1,0:T(8,128)S(1)}, u32[]{:S(2)}, u32[]{:S(2)}) async-start(f32[64,32,128]{2,1,0:T(8,128)} %pad_maximum_fusion), calls=%async_computation.1 | async-start | bytes 2097152 | tf_op jit(solution)/shard_map/all_to_all | solution.py:273
  50.5 60.0 %all-to-all-start = ((f32[128,65,1,128]{3,2,1,0:T(1,128)}), f32[128,65,1,128]{3,2,1,0:T(1,128)}, u32[]{:S(2)}, u32[]{:S(2)}) async-start(f32[128,65,1,128]{3,2,1,0:T(1,128)} %bitcast.5), calls=%async_computation | async-start | bytes 8519680 | tf_op jit(solution)/shard_map/all_to_all | solution.py:267

commit v4 on v3

--- a/solution.py
+++ b/solution.py
@@ -180,7 +180,7 @@
     )(recv)
 
 
-def heavy_kernel(values, keys, heavy_ids, core, owners):
+def heavy_kernel(values, keys, heavy_ids, place, owners, across):
     events, width = values.shape
     heavy = heavy_ids.shape[0]
     tile = heavy // 2
@@ -188,15 +188,18 @@
     event_rows = events // LANES
     rows = step_events // LANES
     half = owners // 2
+    stride = half // across
     piece = heavy // owners
 
-    def body(core_ref, h_ref, k_ref, v_ref, near_ref, far_ref, ids, rhs):
+    def body(at_ref, h_ref, k_ref, v_ref, near_ref, far_ref, ids, rhs):
         c = pl.program_id(0)
 
         @pl.when(c == 0)
         def _():
             for p in range(owners):
-                source = (p % half) * 2 + (core_ref[0] + p // half) % 2
+                x = (at_ref[0] + p % half // stride) % (half // stride)
+                core = (at_ref[1] + p // half) % 2
+                source = (x * stride + p % stride) * 2 + core
                 column = h_ref[pl.ds(pl.multiple_of(source * piece, piece), piece), :]
                 ids[pl.ds(p * piece, piece), :] = jnp.broadcast_to(column, (piece, LANES))
 
@@ -255,7 +258,7 @@
             pltpu.VMEM((events, 2 * width), jnp.bfloat16),
         ],
         name="heavy_sums",
-    )(core, heavy_ids.reshape(heavy, 1), keys.reshape(event_rows, LANES), values)
+    )(place, heavy_ids.reshape(heavy, 1), keys.reshape(event_rows, LANES), values)
 
 
 def per_device(values, key_ids, heavy_ids, block_offsets, block_counts):
@@ -265,12 +268,19 @@
     packed = pack_blocks(block_offsets, block_counts, key_ids, values, sizes)
     order = ("z", "y_hi", "rep", "x", "core")
     recv = lax.all_to_all(packed, order, split_axis=0, concat_axis=0, tiled=True)
-    core = lax.axis_index("core").astype(jnp.int32).reshape(1)
-    near, far = heavy_kernel(values, key_ids, heavy_ids, core, owners)
+    across = lax.axis_size("x")
+    place = jnp.stack([lax.axis_index("x"), lax.axis_index("core")]).astype(jnp.int32)
+    near, far = heavy_kernel(values, key_ids, heavy_ids, place, owners, across)
+    width = near.shape[1]
     near = near + lax.ppermute(far, "core", [(0, 1), (1, 0)])
-    pieces = near.reshape(owners // 2, -1, near.shape[1])
+    parts = near.reshape(across, -1, width)
+    near = parts[0]
+    for d in range(1, across):
+        ring = [(i, (i + d) % across) for i in range(across)]
+        near = near + lax.ppermute(parts[d], "x", ring)
+    pieces = near.reshape(owners // 2 // across, -1, width)
     pieces = jnp.concatenate([pieces, pieces], axis=0)
-    pieces = lax.all_to_all(pieces, ("rep", "x", "z", "y_hi"), 0, 0, tiled=True)
+    pieces = lax.all_to_all(pieces, ("rep", "z", "y_hi"), 0, 0, tiled=True)
     light_sums = light_kernel(recv)
     heavy_sums = jnp.sum(pieces, axis=0)
     return (light_sums, heavy_sums)

time: 123 us -> 122 us (level)
    all_to_all x1, waiting for transfers between devices: 12.3 us -> 2.6 us  [per_device(): pieces = lax.all_to_all(pieces, ('rep', 'z', 'y_hi'), 0, 0, tiled=True)]
    ppermute x0 -> x3, waiting for transfers between devices: none -> 8.6 us  [per_device(): near = near + lax.ppermute(parts[d], 'x', ring)]
    ppermute x0 -> x3, starting transfers between devices: none -> 3.78 us  [per_device(): near = near + lax.ppermute(parts[d], 'x', ring)]
    all_to_all x1, starting transfers between devices: 11.2 us -> 7.77 us  [per_device(): pieces = lax.all_to_all(pieces, ('rep', 'z', 'y_hi'), 0, 0, tiled=True)]
  transfers between devices with their start and end apart: 3 -> 6, of which waited for: 3 -> 6; matrix products, arithmetic and copies ran while one was open for 1% -> 1% of each run, Pallas kernels for 4% -> 4%
where the time goes in v4:
time: 122 us
  waiting for transfers between devices  65.8 us (54%)
  Pallas kernels  30.6 us (25%)
  starting transfers between devices  19.3 us (16%)
  other arithmetic  3.15 us (3%)
  local copies, waits for them, and re-layouts  2.06 us (2%)
    all_to_all x1, waiting for transfers between devices, per_device(): lax.all_to_all(packed, order, split_axis=0, concat_axis=0, tiled=True)  52.8 us
    pallas_call x1, Pallas kernels, heavy_kernel(): pl.pallas_call(body, grid=(2,), out_shape=(side, side), in_specs=[pl.Bloc...  13.8 us
    pallas_call x1, Pallas kernels, light_kernel(): pl.pallas_call(body, out_shape=jax.ShapeDtypeStruct((KEYS_DEV, width), jn...  11.8 us
    ppermute x3, waiting for transfers between devices, per_device(): near = near + lax.ppermute(parts[d], 'x', ring)  8.6 us
    all_to_all x1, starting transfers between devices, per_device(): pieces = lax.all_to_all(pieces, ('rep', 'z', 'y_hi'), 0, 0, tiled=True)  7.77 us
    all_to_all x1, starting transfers between devices, per_device(): lax.all_to_all(packed, order, split_axis=0, concat_axis=0, tiled=True)  6.34 us
    pallas_call x1, Pallas kernels, pack_blocks(): pl.pallas_call(body, out_shape=jax.ShapeDtypeStruct((groups * nr, members...  5.12 us
    ppermute x3, starting transfers between devices, per_device(): near = near + lax.ppermute(parts[d], 'x', ring)  3.78 us
  transfers between devices with their start and end apart: 6, of which 6 were waited for; matrix products, arithmetic and copies ran while one was open for 1% of the time, Pallas kernels for 4%

profile of v4, /device:TPU:1, one launch (start us, length us, event | category | flops | bytes accessed | tf_op | source)
XLA Modules:
  0.0 121.6 jit_solution(10240638811124850609)
XLA Ops:
  0.6 2.0 %copy.7.h_ref = s32[2048,1]{1,0:T(8,128)} copy(s32[2048,1]{0,1:T(1,128)} %bitcast.10) | data formatting | bytes 16384 | tf_op jit(solution)/shard_map/reshape | solution.py:261
  2.7 0.6 pad_add_fusion.at_ref
  3.3 13.8 %heavy_sums.1 = (f32[1024,128]{1,0:T(8,128)}, f32[1024,128]{1,0:T(8,128)}) custom-call(s32[2]{0:T(128)} %pad_add_fusion.at_ref, s32[2048,1]{1,0:T(8,128)} %copy.7.h_ref, s32[64,128]{1,0:T(8,128)} %bitcast.8, f32[8192,128]{1,0:T(8,128)} %v_ref.1), custom_call_target="tpu_custom_call" | custom-call | tf_op jit(solution)/shard_map/heavy_sums/pallas_call | solution.py:242
  17.1 1.4 %collective-permute-start = (f32[1024,128]{1,0:T(8,128)}, f32[1024,128]{1,0:T(8,128)S(1)}, u32[]{:S(2)}, u32[]{:S(2)}) collective-permute-start(f32[1024,128]{1,0:T(8,128)} %get-tuple-element.5), channel_id=1, source_target_pairs={{0,1},{1,0},{2,3},{3,2},{4,5},{5,4},{6,7},{7,6},{8,9},{9,8},{10,11... | collective-permute-start | bytes 1572872 | tf_op jit(solution)/shard_map/ppermute | solution.py:275
  18.5 1.7 %collective-permute-done = f32[1024,128]{1,0:T(8,128)S(1)} collective-permute-done((f32[1024,128]{1,0:T(8,128)}, f32[1024,128]{1,0:T(8,128)S(1)}, u32[]{:S(2)}, u32[]{:S(2)}) %collective-permute-start) | collective-permute-done | bytes 524320 | tf_op jit(solution)/shard_map/ppermute | solution.py:275
  20.2 1.1 add.12
  21.4 2.7 %collective-permute-start.3 = (f32[256,128]{1,0:T(8,128)S(1)}, f32[256,128]{1,0:T(8,128)S(1)}, u32[]{:S(2)}, u32[]{:S(2)}) collective-permute-start(f32[256,128]{1,0:T(8,128)S(1)} %get-tuple-element.7), channel_id=1, source_target_pairs={{0,48},{16,0},{32,16},{48,32},{1,49},{17,1},{33,17},{49,33},{2,50}... | collective-permute-start | bytes 393224 | tf_op jit(solution)/shard_map/ppermute | solution.py:280
  24.0 0.5 collective-permute-start.2
  24.5 0.6 collective-permute-start.1
  25.1 4.0 %collective-permute-done.3 = f32[256,128]{1,0:T(8,128)S(1)} collective-permute-done((f32[256,128]{1,0:T(8,128)S(1)}, f32[256,128]{1,0:T(8,128)S(1)}, u32[]{:S(2)}, u32[]{:S(2)}) %collective-permute-start.3) | collective-permute-done | bytes 131104 | tf_op jit(solution)/shard_map/ppermute | solution.py:280
  29.2 0.8 collective-permute-done.2
  29.9 3.8 %collective-permute-done.1 = f32[256,128]{1,0:T(8,128)S(1)} collective-permute-done((f32[256,128]{1,0:T(8,128)S(1)}, f32[256,128]{1,0:T(8,128)S(1)}, u32[]{:S(2)}, u32[]{:S(2)}) %collective-permute-start.1) | collective-permute-done | bytes 131104 | tf_op jit(solution)/shard_map/ppermute | solution.py:280
  33.8 0.7 pad_maximum_fusion
  34.5 7.8 %all-to-all-start.1 = ((f32[16,32,128]{2,1,0:T(8,128)}), f32[16,32,128]{2,1,0:T(8,128)S(1)}, u32[]{:S(2)}, u32[]{:S(2)}) async-start(f32[16,32,128]{2,1,0:T(8,128)} %pad_maximum_fusion), calls=%async_computation.1 | async-start | bytes 524288 | tf_op jit(solution)/shard_map/all_to_all | solution.py:283
  42.3 5.1 %pack_blocks.1 = f32[16,520,128]{2,1,0:T(8,128)} custom-call(s32[1,64]{1,0:T(1,128)} %off_ref.1, s32[1,64]{1,0:T(1,128)} %cnt_ref.1, s32[64,128]{1,0:T(8,128)} %bitcast.9, f32[8192,128]{1,0:T(8,128)} %v_ref.1), custom_call_target="tpu_custom_call" | custom-call | tf_op jit(solution)/shard_map/pack_blocks/pallas_call | solution.py:74
  47.4 2.6 %all-to-all-done.1 = f32[16,32,128]{2,1,0:T(8,128)S(1)} async-done(((f32[16,32,128]{2,1,0:T(8,128)}), f32[16,32,128]{2,1,0:T(8,128)S(1)}, u32[]{:S(2)}, u32[]{:S(2)}) %all-to-all-start.1) | async-done | bytes 262176 | tf_op jit(solution)/shard_map/all_to_all | solution.py:283
  50.0 6.3 %all-to-all-start = ((f32[128,65,1,128]{3,2,1,0:T(1,128)}), f32[128,65,1,128]{3,2,1,0:T(1,128)}, u32[]{:S(2)}, u32[]{:S(2)}) async-start(f32[128,65,1,128]{3,2,1,0:T(1,128)} %bitcast.6), calls=%async_computation | async-start | bytes 8519680 | tf_op jit(solution)/shard_map/all_to_all | solution.py:270
  56.3 0.6 reduce_sum.9
  57.0 52.8 %all-to-all-done.recv_ref = f32[128,65,1,128]{3,2,1,0:T(1,128)} async-done(((f32[128,65,1,128]{3,2,1,0:T(1,128)}), f32[128,65,1,128]{3,2,1,0:T(1,128)}, u32[]{:S(2)}, u32[]{:S(2)}) %all-to-all-start) | async-done | bytes 4259872 | tf_op jit(solution)/shard_map/all_to_all | solution.py:270
  109.8 11.8 %light_sums.1 = f32[4096,128]{1,0:T(8,128)} custom-call(f32[128,65,1,128]{3,2,1,0:T(1,128)} %all-to-all-done.recv_ref), custom_call_target="tpu_custom_call" | custom-call | tf_op jit(solution)/shard_map/light_sums/pallas_call | solution.py:162
  (2 shorter events, 0.1 us)
Async XLA Ops:
  17.1 3.1 %collective-permute-start = (f32[1024,128]{1,0:T(8,128)}, f32[1024,128]{1,0:T(8,128)S(1)}, u32[]{:S(2)}, u32[]{:S(2)}) collective-permute-start(f32[1024,128]{1,0:T(8,128)} %get-tuple-element.5), channel_id=1, source_target_pairs={{0,1},{1,0},{2,3},{3,2},{4,5},{5,4},{6,7},{7,6},{8,9},{9,8},{10,11... | collective-permute-start | bytes 1572872 | tf_op jit(solution)/shard_map/ppermute | solution.py:275
  21.4 7.8 %collective-permute-start.3 = (f32[256,128]{1,0:T(8,128)S(1)}, f32[256,128]{1,0:T(8,128)S(1)}, u32[]{:S(2)}, u32[]{:S(2)}) collective-permute-start(f32[256,128]{1,0:T(8,128)S(1)} %get-tuple-element.7), channel_id=1, source_target_pairs={{0,48},{16,0},{32,16},{48,32},{1,49},{17,1},{33,17},{49,33},{2,50}... | collective-permute-start | bytes 393224 | tf_op jit(solution)/shard_map/ppermute | solution.py:280
  24.0 5.9 %collective-permute-start.2 = (f32[256,128]{1,0:T(8,128)S(1)}, f32[256,128]{1,0:T(8,128)S(1)}, u32[]{:S(2)}, u32[]{:S(2)}) collective-permute-start(f32[256,128]{1,0:T(8,128)S(1)} %get-tuple-element.8), channel_id=1, source_target_pairs={{0,32},{16,48},{32,0},{48,16},{1,33},{17,49},{33,1},{49,17},{2,34}... | collective-permute-start | bytes 393224 | tf_op jit(solution)/shard_map/ppermute | solution.py:280
  24.5 9.2 %collective-permute-start.1 = (f32[256,128]{1,0:T(8,128)S(1)}, f32[256,128]{1,0:T(8,128)S(1)}, u32[]{:S(2)}, u32[]{:S(2)}) collective-permute-start(f32[256,128]{1,0:T(8,128)S(1)} %get-tuple-element.6), channel_id=1, source_target_pairs={{0,16},{16,32},{32,48},{48,0},{1,17},{17,33},{33,49},{49,1},{2,18}... | collective-permute-start | bytes 393224 | tf_op jit(solution)/shard_map/ppermute | solution.py:280
  34.5 15.5 %all-to-all-start.1 = ((f32[16,32,128]{2,1,0:T(8,128)}), f32[16,32,128]{2,1,0:T(8,128)S(1)}, u32[]{:S(2)}, u32[]{:S(2)}) async-start(f32[16,32,128]{2,1,0:T(8,128)} %pad_maximum_fusion), calls=%async_computation.1 | async-start | bytes 524288 | tf_op jit(solution)/shard_map/all_to_all | solution.py:283
  50.0 59.8 %all-to-all-start = ((f32[128,65,1,128]{3,2,1,0:T(1,128)}), f32[128,65,1,128]{3,2,1,0:T(1,128)}, u32[]{:S(2)}, u32[]{:S(2)}) async-start(f32[128,65,1,128]{3,2,1,0:T(1,128)} %bitcast.6), calls=%async_computation | async-start | bytes 8519680 | tf_op jit(solution)/shard_map/all_to_all | solution.py:270

commit v5 on v4

--- a/solution.py
+++ b/solution.py
@@ -10,6 +10,7 @@
 LANES = 128
 BANKS = 8
 CHUNK = 32
+HALF = 32
 
 
 def pack_blocks(offs, cnts, keys, values, sizes):
@@ -23,7 +24,7 @@
     def owner_of(g, m):
         return (((m // nc) * nz + g // ny) * ny + g % ny) * nc + m % nc
 
-    def body(off_ref, cnt_ref, keys_ref, val_ref, out_ref, rows, buf, krow, arow, in_sem, out_sem):
+    def body(off_ref, cnt_ref, keys_ref, val_ref, out_ref, rows, buf, krow, arow, last, in_sem, out_sem):
         lane = lax.broadcasted_iota(jnp.int32, (1, LANES), 1)
 
         load = pltpu.make_async_copy(val_ref, rows, in_sem)
@@ -43,6 +44,7 @@
             inside = (pos >= off) & (pos < end)
             krow[pl.ds(b, 1), :] = jnp.where(inside, key - o * KEYS_DEV, KEYS_DEV)
             arow[pl.ds(b, 1), :] = jnp.full((1, LANES), shift, jnp.int32)
+            last[pl.ds(b, 1), :] = jnp.full((1, LANES), end - start, jnp.int32)
             return carry
 
         lax.fori_loop(0, owners, block_keys, 0, unroll=16)
@@ -51,7 +53,8 @@
         for bit in range(7):
             moved = pltpu.roll(rolled, LANES - (1 << bit), 1)
             rolled = jnp.where((shifts >> bit) & 1 == 1, moved, rolled)
-        krow[...] = rolled
+        lanes = lax.broadcasted_iota(jnp.int32, rolled.shape, 1)
+        krow[...] = jnp.where(lanes == CAP, last[...], rolled)
         load.wait()
         stores = []
         for g in range(groups):
@@ -86,6 +89,7 @@
             pltpu.VMEM((owners * block, width), jnp.float32),
             pltpu.VMEM((owners, LANES), jnp.int32),
             pltpu.VMEM((owners, LANES), jnp.int32),
+            pltpu.VMEM((owners, LANES), jnp.int32),
             pltpu.SemaphoreType.DMA,
             pltpu.SemaphoreType.DMA((groups * nr,)),
         ],
@@ -110,15 +114,6 @@
                 pltpu.make_async_copy(recv_ref.at[part], rows.at[part], row_sems.at[c])
             )
             copies[c].start()
-        key_copy.wait()
-
-        def convert(i, carry):
-            kint[i] = rows[i, CAP].astype(jnp.int32)
-            return carry
-
-        lax.fori_loop(0, senders, convert, 0, unroll=8)
-        smem_copy = pltpu.make_async_copy(kint, ksm, smem_sem)
-        smem_copy.start()
         zeros = jnp.zeros((64, width), jnp.float32)
 
         def clear(i, carry):
@@ -126,19 +121,53 @@
                 bank[pl.ds(i * 64, 64), :] = zeros
             return carry
 
-        lax.fori_loop(0, KEYS_DEV // 64, clear, 0)
+        def convert(i, longer):
+            keys = rows[i, CAP].astype(jnp.int32)
+            kint[i] = keys
+            return longer + jnp.where(keys > HALF, 1, 0)
+
+        spans = KEYS_DEV // 64
+        lax.fori_loop(0, spans * 5 // 8, clear, 0)
+        key_copy.wait()
+        longer = jnp.zeros((1, width), jnp.int32)
+        longer = lax.fori_loop(0, senders, convert, longer, unroll=8)
+        smem_copy = pltpu.make_async_copy(kint, ksm, smem_sem)
+        smem_copy.start()
+        lane = lax.broadcasted_iota(jnp.int32, (1, width), 1)
+        full = jnp.sum(jnp.where(lane == CAP, longer, 0)) * 2 > senders
+        lax.fori_loop(spans * 5 // 8, spans, clear, 0)
         smem_copy.wait()
 
-        def sender(i, carry):
-            for s in range(CAP):
+        def add_slots(i, slots):
+            for s in slots:
                 bank = acc[s % BANKS]
                 key = ksm[i, 0, s]
                 bank[pl.ds(key, 1), :] = bank[pl.ds(key, 1), :] + rows[i, s]
+
+        def sender(i, carry):
+            add_slots(i, range(CAP))
+            return carry
+
+        def short_sender(i, carry):
+            add_slots(i, range(HALF))
+
+            @pl.when(ksm[i, 0, CAP] > HALF)
+            def _():
+                add_slots(i, range(HALF, CAP))
+
             return carry
 
         for c in range(chunks):
             copies[c].wait()
-            lax.fori_loop(c * CHUNK, (c + 1) * CHUNK, sender, 0)
+
+            @pl.when(full)
+            def _():
+                lax.fori_loop(c * CHUNK, (c + 1) * CHUNK, sender, 0, unroll=4)
+
+            @pl.when(jnp.logical_not(full))
+            def _():
+                lax.fori_loop(c * CHUNK, (c + 1) * CHUNK, short_sender, 0, unroll=4)
+
 
         def finish(i, carry):
             span = pl.ds(i * 64, 64)

time: 122 us -> 121 us (level)
  Pallas kernels: 30.6 us -> 29.1 us
    pallas_call x1, Pallas kernels: 11.8 us -> 10.2 us  [light_kernel(): pl.pallas_call(body, out_shape=jax.ShapeDtypeStruct((KEYS_DEV, width), jn...]
where the time goes in v5:
time: 121 us; the launch traced here: 120 us
  waiting for transfers between devices  65.8 us (54%)
  Pallas kernels  29.1 us (24%)
  starting transfers between devices  19.3 us (16%)
  other arithmetic  3.15 us (3%)
  local copies, waits for them, and re-layouts  2.06 us (2%)
    all_to_all x1, waiting for transfers between devices, per_device(): lax.all_to_all(packed, order, split_axis=0, concat_axis=0, tiled=True)  52.8 us
    pallas_call x1, Pallas kernels, heavy_kernel(): pl.pallas_call(body, grid=(2,), out_shape=(side, side), in_specs=[pl.Bloc...  13.8 us
    pallas_call x1, Pallas kernels, light_kernel(): pl.pallas_call(body, out_shape=jax.ShapeDtypeStruct((KEYS_DEV, width), jn...  10.2 us
    ppermute x3, waiting for transfers between devices, per_device(): near = near + lax.ppermute(parts[d], 'x', ring)  8.6 us
    all_to_all x1, starting transfers between devices, per_device(): pieces = lax.all_to_all(pieces, ('rep', 'z', 'y_hi'), 0, 0, tiled=True)  7.77 us
    all_to_all x1, starting transfers between devices, per_device(): lax.all_to_all(packed, order, split_axis=0, concat_axis=0, tiled=True)  6.34 us
    pallas_call x1, Pallas kernels, pack_blocks(): pl.pallas_call(body, out_shape=jax.ShapeDtypeStruct((groups * nr, members...  5.12 us
    ppermute x3, starting transfers between devices, per_device(): near = near + lax.ppermute(parts[d], 'x', ring)  3.78 us
  transfers between devices with their start and end apart: 6, of which 6 were waited for; matrix products, arithmetic and copies ran while one was open for 1% of the time, Pallas kernels for 4%

profile of v5, /device:TPU:1, one launch (start us, length us, event | category | flops | bytes accessed | tf_op | source)
XLA Modules:
  0.0 120.0 jit_solution(6933416608531830534)
XLA Ops:
  0.6 2.0 %copy.7.h_ref = s32[2048,1]{1,0:T(8,128)} copy(s32[2048,1]{0,1:T(1,128)} %bitcast.10) | data formatting | bytes 16384 | tf_op jit(solution)/shard_map/reshape | solution.py:290
  2.7 0.6 pad_add_fusion.at_ref
  3.3 13.8 %heavy_sums.1 = (f32[1024,128]{1,0:T(8,128)}, f32[1024,128]{1,0:T(8,128)}) custom-call(s32[2]{0:T(128)} %pad_add_fusion.at_ref, s32[2048,1]{1,0:T(8,128)} %copy.7.h_ref, s32[64,128]{1,0:T(8,128)} %bitcast.8, f32[8192,128]{1,0:T(8,128)} %v_ref.1), custom_call_target="tpu_custom_call" | custom-call | tf_op jit(solution)/shard_map/heavy_sums/pallas_call | solution.py:271
  17.1 1.4 %collective-permute-start = (f32[1024,128]{1,0:T(8,128)}, f32[1024,128]{1,0:T(8,128)S(1)}, u32[]{:S(2)}, u32[]{:S(2)}) collective-permute-start(f32[1024,128]{1,0:T(8,128)} %get-tuple-element.5), channel_id=1, source_target_pairs={{0,1},{1,0},{2,3},{3,2},{4,5},{5,4},{6,7},{7,6},{8,9},{9,8},{10,11... | collective-permute-start | bytes 1572872 | tf_op jit(solution)/shard_map/ppermute | solution.py:304
  18.5 1.7 %collective-permute-done = f32[1024,128]{1,0:T(8,128)S(1)} collective-permute-done((f32[1024,128]{1,0:T(8,128)}, f32[1024,128]{1,0:T(8,128)S(1)}, u32[]{:S(2)}, u32[]{:S(2)}) %collective-permute-start) | collective-permute-done | bytes 524320 | tf_op jit(solution)/shard_map/ppermute | solution.py:304
  20.2 1.1 add.12
  21.4 2.7 %collective-permute-start.3 = (f32[256,128]{1,0:T(8,128)S(1)}, f32[256,128]{1,0:T(8,128)S(1)}, u32[]{:S(2)}, u32[]{:S(2)}) collective-permute-start(f32[256,128]{1,0:T(8,128)S(1)} %get-tuple-element.7), channel_id=1, source_target_pairs={{0,48},{16,0},{32,16},{48,32},{1,49},{17,1},{33,17},{49,33},{2,50}... | collective-permute-start | bytes 393224 | tf_op jit(solution)/shard_map/ppermute | solution.py:309
  24.0 0.5 collective-permute-start.2
  24.5 0.6 collective-permute-start.1
  25.1 4.0 %collective-permute-done.3 = f32[256,128]{1,0:T(8,128)S(1)} collective-permute-done((f32[256,128]{1,0:T(8,128)S(1)}, f32[256,128]{1,0:T(8,128)S(1)}, u32[]{:S(2)}, u32[]{:S(2)}) %collective-permute-start.3) | collective-permute-done | bytes 131104 | tf_op jit(solution)/shard_map/ppermute | solution.py:309
  29.2 0.8 collective-permute-done.2
  29.9 3.8 %collective-permute-done.1 = f32[256,128]{1,0:T(8,128)S(1)} collective-permute-done((f32[256,128]{1,0:T(8,128)S(1)}, f32[256,128]{1,0:T(8,128)S(1)}, u32[]{:S(2)}, u32[]{:S(2)}) %collective-permute-start.1) | collective-permute-done | bytes 131104 | tf_op jit(solution)/shard_map/ppermute | solution.py:309
  33.8 0.7 pad_maximum_fusion
  34.5 7.8 %all-to-all-start.1 = ((f32[16,32,128]{2,1,0:T(8,128)}), f32[16,32,128]{2,1,0:T(8,128)S(1)}, u32[]{:S(2)}, u32[]{:S(2)}) async-start(f32[16,32,128]{2,1,0:T(8,128)} %pad_maximum_fusion), calls=%async_computation.1 | async-start | bytes 524288 | tf_op jit(solution)/shard_map/all_to_all | solution.py:312
  42.3 5.1 %pack_blocks.1 = f32[16,520,128]{2,1,0:T(8,128)} custom-call(s32[1,64]{1,0:T(1,128)} %off_ref.1, s32[1,64]{1,0:T(1,128)} %cnt_ref.1, s32[64,128]{1,0:T(8,128)} %bitcast.9, f32[8192,128]{1,0:T(8,128)} %v_ref.1), custom_call_target="tpu_custom_call" | custom-call | tf_op jit(solution)/shard_map/pack_blocks/pallas_call | solution.py:77
  47.4 2.6 %all-to-all-done.1 = f32[16,32,128]{2,1,0:T(8,128)S(1)} async-done(((f32[16,32,128]{2,1,0:T(8,128)}), f32[16,32,128]{2,1,0:T(8,128)S(1)}, u32[]{:S(2)}, u32[]{:S(2)}) %all-to-all-start.1) | async-done | bytes 262176 | tf_op jit(solution)/shard_map/all_to_all | solution.py:312
  50.0 6.3 %all-to-all-start = ((f32[128,65,1,128]{3,2,1,0:T(1,128)}), f32[128,65,1,128]{3,2,1,0:T(1,128)}, u32[]{:S(2)}, u32[]{:S(2)}) async-start(f32[128,65,1,128]{3,2,1,0:T(1,128)} %bitcast.6), calls=%async_computation | async-start | bytes 8519680 | tf_op jit(solution)/shard_map/all_to_all | solution.py:299
  56.3 0.6 reduce_sum.9
  57.0 52.8 %all-to-all-done.recv_ref = f32[128,65,1,128]{3,2,1,0:T(1,128)} async-done(((f32[128,65,1,128]{3,2,1,0:T(1,128)}), f32[128,65,1,128]{3,2,1,0:T(1,128)}, u32[]{:S(2)}, u32[]{:S(2)}) %all-to-all-start) | async-done | bytes 4259872 | tf_op jit(solution)/shard_map/all_to_all | solution.py:299
  109.8 10.2 %light_sums.1 = f32[4096,128]{1,0:T(8,128)} custom-call(f32[128,65,1,128]{3,2,1,0:T(1,128)} %all-to-all-done.recv_ref), custom_call_target="tpu_custom_call" | custom-call | tf_op jit(solution)/shard_map/light_sums/pallas_call | solution.py:191
  (2 shorter events, 0.1 us)
Async XLA Ops:
  17.1 3.1 %collective-permute-start = (f32[1024,128]{1,0:T(8,128)}, f32[1024,128]{1,0:T(8,128)S(1)}, u32[]{:S(2)}, u32[]{:S(2)}) collective-permute-start(f32[1024,128]{1,0:T(8,128)} %get-tuple-element.5), channel_id=1, source_target_pairs={{0,1},{1,0},{2,3},{3,2},{4,5},{5,4},{6,7},{7,6},{8,9},{9,8},{10,11... | collective-permute-start | bytes 1572872 | tf_op jit(solution)/shard_map/ppermute | solution.py:304
  21.4 7.8 %collective-permute-start.3 = (f32[256,128]{1,0:T(8,128)S(1)}, f32[256,128]{1,0:T(8,128)S(1)}, u32[]{:S(2)}, u32[]{:S(2)}) collective-permute-start(f32[256,128]{1,0:T(8,128)S(1)} %get-tuple-element.7), channel_id=1, source_target_pairs={{0,48},{16,0},{32,16},{48,32},{1,49},{17,1},{33,17},{49,33},{2,50}... | collective-permute-start | bytes 393224 | tf_op jit(solution)/shard_map/ppermute | solution.py:309
  24.0 5.9 %collective-permute-start.2 = (f32[256,128]{1,0:T(8,128)S(1)}, f32[256,128]{1,0:T(8,128)S(1)}, u32[]{:S(2)}, u32[]{:S(2)}) collective-permute-start(f32[256,128]{1,0:T(8,128)S(1)} %get-tuple-element.8), channel_id=1, source_target_pairs={{0,32},{16,48},{32,0},{48,16},{1,33},{17,49},{33,1},{49,17},{2,34}... | collective-permute-start | bytes 393224 | tf_op jit(solution)/shard_map/ppermute | solution.py:309
  24.5 9.2 %collective-permute-start.1 = (f32[256,128]{1,0:T(8,128)S(1)}, f32[256,128]{1,0:T(8,128)S(1)}, u32[]{:S(2)}, u32[]{:S(2)}) collective-permute-start(f32[256,128]{1,0:T(8,128)S(1)} %get-tuple-element.6), channel_id=1, source_target_pairs={{0,16},{16,32},{32,48},{48,0},{1,17},{17,33},{33,49},{49,1},{2,18}... | collective-permute-start | bytes 393224 | tf_op jit(solution)/shard_map/ppermute | solution.py:309
  34.5 15.5 %all-to-all-start.1 = ((f32[16,32,128]{2,1,0:T(8,128)}), f32[16,32,128]{2,1,0:T(8,128)S(1)}, u32[]{:S(2)}, u32[]{:S(2)}) async-start(f32[16,32,128]{2,1,0:T(8,128)} %pad_maximum_fusion), calls=%async_computation.1 | async-start | bytes 524288 | tf_op jit(solution)/shard_map/all_to_all | solution.py:312
  50.0 59.8 %all-to-all-start = ((f32[128,65,1,128]{3,2,1,0:T(1,128)}), f32[128,65,1,128]{3,2,1,0:T(1,128)}, u32[]{:S(2)}, u32[]{:S(2)}) async-start(f32[128,65,1,128]{3,2,1,0:T(1,128)} %bitcast.6), calls=%async_computation | async-start | bytes 8519680 | tf_op jit(solution)/shard_map/all_to_all | solution.py:299

commit v6 on v5

--- a/solution.py
+++ b/solution.py
@@ -166,7 +166,7 @@
 
             @pl.when(jnp.logical_not(full))
             def _():
-                lax.fori_loop(c * CHUNK, (c + 1) * CHUNK, short_sender, 0, unroll=4)
+                lax.fori_loop(c * CHUNK, (c + 1) * CHUNK, short_sender, 0, unroll=8)
 
 
         def finish(i, carry):
@@ -290,6 +290,27 @@
     )(place, heavy_ids.reshape(heavy, 1), keys.reshape(event_rows, LANES), values)
 
 
+def sum_twice(*parts):
+    count = parts[0].shape[0]
+
+    def body(*refs):
+        total = refs[0][...]
+        for ref in refs[1:-1]:
+            total = total + ref[...]
+        refs[-1][:count] = total
+        refs[-1][count:] = total
+
+    vmem = pl.BlockSpec(memory_space=pltpu.VMEM)
+    return pl.pallas_call(
+        body,
+        out_shape=jax.ShapeDtypeStruct((2 * count,) + parts[0].shape[1:], jnp.float32),
+        in_specs=[vmem] * len(parts),
+        out_specs=vmem,
+        compiler_params=pltpu.CompilerParams(vmem_limit_bytes=4 << 20),
+        name="sum_twice",
+    )(*parts)
+
+
 def per_device(values, key_ids, heavy_ids, block_offsets, block_counts):
     own = ("x", "z", "y_hi", "core")
     sizes = tuple(lax.axis_size(axis) for axis in ("rep",) + own)
@@ -302,13 +323,12 @@
     near, far = heavy_kernel(values, key_ids, heavy_ids, place, owners, across)
     width = near.shape[1]
     near = near + lax.ppermute(far, "core", [(0, 1), (1, 0)])
-    parts = near.reshape(across, -1, width)
-    near = parts[0]
+    parts = near.reshape(across, owners // 2 // across, -1, width)
+    sent = []
     for d in range(1, across):
         ring = [(i, (i + d) % across) for i in range(across)]
-        near = near + lax.ppermute(parts[d], "x", ring)
-    pieces = near.reshape(owners // 2 // across, -1, width)
-    pieces = jnp.concatenate([pieces, pieces], axis=0)
+        sent.append(lax.ppermute(parts[d], "x", ring))
+    pieces = sum_twice(parts[0], *sent)
     pieces = lax.all_to_all(pieces, ("rep", "z", "y_hi"), 0, 0, tiled=True)
     light_sums = light_kernel(recv)
     heavy_sums = jnp.sum(pieces, axis=0)

time: 121 us -> 121 us (level)
  waiting for transfers between devices: 65.8 us -> 61.7 us
  starting transfers between devices: 19.3 us -> 22.4 us
    ppermute x3, waiting for transfers between devices: 8.6 us -> 4.87 us  [per_device(): sent.append(lax.ppermute(parts[d], 'x', ring))]
    all_to_all x1, starting transfers between devices: 6.34 us -> 8.31 us  [per_device(): lax.all_to_all(packed, order, split_axis=0, concat_axis=0, tiled=True)]
    ppermute x3, starting transfers between devices: 3.78 us -> 4.99 us  [per_device(): sent.append(lax.ppermute(parts[d], 'x', ring))]
  transfers between devices with their start and end apart: 6 -> 6, of which waited for: 6 -> 5; matrix products, arithmetic and copies ran while one was open for 1% -> 1% of each run, Pallas kernels for 4% -> 4%
where the time goes in v6:
time: 121 us; the launch traced here: 119 us
  waiting for transfers between devices  61.7 us (51%)
  Pallas kernels  29.7 us (25%)
  starting transfers between devices  22.4 us (19%)
  other arithmetic  2.39 us (2%)
  local copies, waits for them, and re-layouts  2.07 us (2%)
    all_to_all x1, waiting for transfers between devices, per_device(): lax.all_to_all(packed, order, split_axis=0, concat_axis=0, tiled=True)  52.7 us
    pallas_call x1, Pallas kernels, heavy_kernel(): pl.pallas_call(body, grid=(2,), out_shape=(side, side), in_specs=[pl.Bloc...  13.8 us
    pallas_call x1, Pallas kernels, light_kernel(): pl.pallas_call(body, out_shape=jax.ShapeDtypeStruct((KEYS_DEV, width), jn...  10.1 us
    all_to_all x1, starting transfers between devices, per_device(): lax.all_to_all(packed, order, split_axis=0, concat_axis=0, tiled=True)  8.31 us
    all_to_all x1, starting transfers between devices, per_device(): pieces = lax.all_to_all(pieces, ('rep', 'z', 'y_hi'), 0, 0, tiled=True)  7.77 us
    pallas_call x1, Pallas kernels, pack_blocks(): pl.pallas_call(body, out_shape=jax.ShapeDtypeStruct((groups * nr, members...  5.12 us
    ppermute x3, starting transfers between devices, per_device(): sent.append(lax.ppermute(parts[d], 'x', ring))  4.99 us
    ppermute x3, waiting for transfers between devices, per_device(): sent.append(lax.ppermute(parts[d], 'x', ring))  4.87 us
  transfers between devices with their start and end apart: 6, of which 5 were waited for; matrix products, arithmetic and copies ran while one was open for 1% of the time, Pallas kernels for 4%

profile of v6, /device:TPU:1, one launch (start us, length us, event | category | flops | bytes accessed | tf_op | source)
XLA Modules:
  0.0 119.1 jit_solution(4403123773934446729)
XLA Ops:
  0.6 2.0 %copy.7.h_ref = s32[2048,1]{1,0:T(8,128)} copy(s32[2048,1]{0,1:T(1,128)} %bitcast.16) | data formatting | bytes 16384 | tf_op jit(solution)/shard_map/reshape | solution.py:290
  2.7 0.6 pad_add_fusion.at_ref
  3.3 13.8 %heavy_sums.1 = (f32[1024,128]{1,0:T(8,128)}, f32[1024,128]{1,0:T(8,128)}) custom-call(s32[2]{0:T(128)} %pad_add_fusion.at_ref, s32[2048,1]{1,0:T(8,128)} %copy.7.h_ref, s32[64,128]{1,0:T(8,128)} %bitcast.11, f32[8192,128]{1,0:T(8,128)} %v_ref.1), custom_call_target="tpu_custom_call" | custom-call | tf_op jit(solution)/shard_map/heavy_sums/pallas_call | solution.py:271
  17.1 1.4 %collective-permute-start = (f32[1024,128]{1,0:T(8,128)}, f32[1024,128]{1,0:T(8,128)S(1)}, u32[]{:S(2)}, u32[]{:S(2)}) collective-permute-start(f32[1024,128]{1,0:T(8,128)} %get-tuple-element.5), channel_id=1, source_target_pairs={{0,1},{1,0},{2,3},{3,2},{4,5},{5,4},{6,7},{7,6},{8,9},{9,8},{10,11... | collective-permute-start | bytes 1572872 | tf_op jit(solution)/shard_map/ppermute | solution.py:325
  18.5 1.7 %collective-permute-done = f32[1024,128]{1,0:T(8,128)S(1)} collective-permute-done((f32[1024,128]{1,0:T(8,128)}, f32[1024,128]{1,0:T(8,128)S(1)}, u32[]{:S(2)}, u32[]{:S(2)}) %collective-permute-start) | collective-permute-done | bytes 524320 | tf_op jit(solution)/shard_map/ppermute | solution.py:325
  20.2 1.1 add.3
  21.4 1.4 %collective-permute-start.1 = (f32[8,32,128]{2,1,0:T(8,128)S(1)}, f32[8,32,128]{2,1,0:T(8,128)S(1)}, u32[]{:S(2)}, u32[]{:S(2)}) collective-permute-start(f32[8,32,128]{2,1,0:T(8,128)S(1)} %bitcast.15), channel_id=1, source_target_pairs={{0,16},{16,32},{32,48},{48,0},{1,17},{17,33},{33,49},{49,1},{2,18}... | collective-permute-start | bytes 393224 | tf_op jit(solution)/shard_map/ppermute | solution.py:330
  22.8 2.4 %collective-permute-start.2 = (f32[8,32,128]{2,1,0:T(8,128)S(1)}, f32[8,32,128]{2,1,0:T(8,128)S(1)}, u32[]{:S(2)}, u32[]{:S(2)}) collective-permute-start(f32[8,32,128]{2,1,0:T(8,128)S(1)} %bitcast.14), channel_id=1, source_target_pairs={{0,32},{16,48},{32,0},{48,16},{1,33},{17,49},{33,1},{49,17},{2,34}... | collective-permute-start | bytes 393224 | tf_op jit(solution)/shard_map/ppermute | solution.py:330
  25.2 1.2 collective-permute-start.3
  26.4 1.0 collective-permute-done.1.refs_1_
  27.3 3.9 %collective-permute-done.2.refs_2_ = f32[8,32,128]{2,1,0:T(8,128)S(1)} collective-permute-done((f32[8,32,128]{2,1,0:T(8,128)S(1)}, f32[8,32,128]{2,1,0:T(8,128)S(1)}, u32[]{:S(2)}, u32[]{:S(2)}) %collective-permute-start.2) | collective-permute-done | bytes 131104 | tf_op jit(solution)/shard_map/ppermute | solution.py:330
  31.2 0.0 collective-permute-done.3.refs_3_
  31.2 0.7 sum_twice.1
  32.0 7.8 %all-to-all-start.1 = ((f32[16,32,128]{2,1,0:T(8,128)}), f32[16,32,128]{2,1,0:T(8,128)S(1)}, u32[]{:S(2)}, u32[]{:S(2)}) async-start(f32[16,32,128]{2,1,0:T(8,128)} %sum_twice.1), calls=%async_computation.1 | async-start | bytes 524288 | tf_op jit(solution)/shard_map/all_to_all | solution.py:332
  39.7 5.1 %pack_blocks.1 = f32[16,520,128]{2,1,0:T(8,128)} custom-call(s32[1,64]{1,0:T(1,128)} %off_ref.1, s32[1,64]{1,0:T(1,128)} %cnt_ref.1, s32[64,128]{1,0:T(8,128)} %bitcast.12, f32[8192,128]{1,0:T(8,128)} %v_ref.1), custom_call_target="tpu_custom_call" | custom-call | tf_op jit(solution)/shard_map/pack_blocks/pallas_call | solution.py:77
  44.9 2.4 %all-to-all-done.1 = f32[16,32,128]{2,1,0:T(8,128)S(1)} async-done(((f32[16,32,128]{2,1,0:T(8,128)}), f32[16,32,128]{2,1,0:T(8,128)S(1)}, u32[]{:S(2)}, u32[]{:S(2)}) %all-to-all-start.1) | async-done | bytes 262176 | tf_op jit(solution)/shard_map/all_to_all | solution.py:332
  47.3 8.3 %all-to-all-start = ((f32[128,65,1,128]{3,2,1,0:T(1,128)}), f32[128,65,1,128]{3,2,1,0:T(1,128)}, u32[]{:S(2)}, u32[]{:S(2)}) async-start(f32[128,65,1,128]{3,2,1,0:T(1,128)} %bitcast.10), calls=%async_computation | async-start | bytes 8519680 | tf_op jit(solution)/shard_map/all_to_all | solution.py:320
  55.6 0.6 reduce_sum.9
  56.2 52.7 %all-to-all-done.recv_ref = f32[128,65,1,128]{3,2,1,0:T(1,128)} async-done(((f32[128,65,1,128]{3,2,1,0:T(1,128)}), f32[128,65,1,128]{3,2,1,0:T(1,128)}, u32[]{:S(2)}, u32[]{:S(2)}) %all-to-all-start) | async-done | bytes 4259872 | tf_op jit(solution)/shard_map/all_to_all | solution.py:320
  108.9 10.1 %light_sums.1 = f32[4096,128]{1,0:T(8,128)} custom-call(f32[128,65,1,128]{3,2,1,0:T(1,128)} %all-to-all-done.recv_ref), custom_call_target="tpu_custom_call" | custom-call | tf_op jit(solution)/shard_map/light_sums/pallas_call | solution.py:191
  (1 shorter events, 0.0 us)
Async XLA Ops:
  17.1 3.1 %collective-permute-start = (f32[1024,128]{1,0:T(8,128)}, f32[1024,128]{1,0:T(8,128)S(1)}, u32[]{:S(2)}, u32[]{:S(2)}) collective-permute-start(f32[1024,128]{1,0:T(8,128)} %get-tuple-element.5), channel_id=1, source_target_pairs={{0,1},{1,0},{2,3},{3,2},{4,5},{5,4},{6,7},{7,6},{8,9},{9,8},{10,11... | collective-permute-start | bytes 1572872 | tf_op jit(solution)/shard_map/ppermute | solution.py:325
  21.4 6.0 %collective-permute-start.1 = (f32[8,32,128]{2,1,0:T(8,128)S(1)}, f32[8,32,128]{2,1,0:T(8,128)S(1)}, u32[]{:S(2)}, u32[]{:S(2)}) collective-permute-start(f32[8,32,128]{2,1,0:T(8,128)S(1)} %bitcast.15), channel_id=1, source_target_pairs={{0,16},{16,32},{32,48},{48,0},{1,17},{17,33},{33,49},{49,1},{2,18}... | collective-permute-start | bytes 393224 | tf_op jit(solution)/shard_map/ppermute | solution.py:330
  22.8 8.5 %collective-permute-start.2 = (f32[8,32,128]{2,1,0:T(8,128)S(1)}, f32[8,32,128]{2,1,0:T(8,128)S(1)}, u32[]{:S(2)}, u32[]{:S(2)}) collective-permute-start(f32[8,32,128]{2,1,0:T(8,128)S(1)} %bitcast.14), channel_id=1, source_target_pairs={{0,32},{16,48},{32,0},{48,16},{1,33},{17,49},{33,1},{49,17},{2,34}... | collective-permute-start | bytes 393224 | tf_op jit(solution)/shard_map/ppermute | solution.py:330
  25.2 6.0 %collective-permute-start.3 = (f32[8,32,128]{2,1,0:T(8,128)S(1)}, f32[8,32,128]{2,1,0:T(8,128)S(1)}, u32[]{:S(2)}, u32[]{:S(2)}) collective-permute-start(f32[8,32,128]{2,1,0:T(8,128)S(1)} %bitcast.13), channel_id=1, source_target_pairs={{0,48},{16,0},{32,16},{48,32},{1,49},{17,1},{33,17},{49,33},{2,50}... | collective-permute-start | bytes 393224 | tf_op jit(solution)/shard_map/ppermute | solution.py:330
  32.0 15.3 %all-to-all-start.1 = ((f32[16,32,128]{2,1,0:T(8,128)}), f32[16,32,128]{2,1,0:T(8,128)S(1)}, u32[]{:S(2)}, u32[]{:S(2)}) async-start(f32[16,32,128]{2,1,0:T(8,128)} %sum_twice.1), calls=%async_computation.1 | async-start | bytes 524288 | tf_op jit(solution)/shard_map/all_to_all | solution.py:332
  47.3 61.7 %all-to-all-start = ((f32[128,65,1,128]{3,2,1,0:T(1,128)}), f32[128,65,1,128]{3,2,1,0:T(1,128)}, u32[]{:S(2)}, u32[]{:S(2)}) async-start(f32[128,65,1,128]{3,2,1,0:T(1,128)} %bitcast.10), calls=%async_computation | async-start | bytes 8519680 | tf_op jit(solution)/shard_map/all_to_all | solution.py:320
